TPU v7x, 256 devices: a whole 4x4x8 slice. The times are simulated.
256 devices in a mesh: section: 2 (over core), fsdp: 8 (over y, x_hi), tp: 16 (over z, x_lo).
Axes of the slice: x: 4 (x_hi: 2, x_lo: 2; x = x_hi * 2 + x_lo), y: 4, z: 8, core: 2. Of those that a mesh axis runs over, the one named last changes fastest.
Arguments:
- saved_inputs: bfloat16 [2, 8, 512, 2560], P('section', None, 'fsdp', 'tp'), may hold values from -6 to 6
- top_grad: bfloat16 [8, 512, 2560], P(None, 'fsdp', 'tp'), may hold values from -6 to 6
- norm_gain: float32 [2, 2560], P('section'), may hold values from 0.5 to 1.5
- gate_weight: bfloat16 [2, 2560, 6912], P('section', 'fsdp', 'tp'), may hold values from -0.125 to 0.125
- up_weight: bfloat16 [2, 2560, 6912], P('section', 'fsdp', 'tp'), may hold values from -0.125 to 0.125
- down_weight: bfloat16 [2, 6912, 2560], P('section', 'tp', 'fsdp'), may hold values from -0.078125 to 0.078125
Outputs:
- input_grads: bfloat16 [2, 8, 512, 2560], P('section', None, 'fsdp', 'tp')
- gate_grad: float32 [2, 2560, 6912], P('section', 'fsdp', 'tp')
- up_grad: float32 [2, 2560, 6912], P('section', 'fsdp', 'tp')
- down_grad: float32 [2, 6912, 2560], P('section', 'tp', 'fsdp')
- gain_grad: float32 [2, 2560], P('section', 'tp')
All inputs are finite; a program needn't handle non-finite values.
Results may differ from a plain program's by a relative error of at most 0.0055.
Values may be sent and summed in bfloat16 or wider, within the bound.
A program may use at most 128 MiB of HBM per device.

v0:
```python
import functools

import jax
import jax.numpy as jnp
from jax import lax
from jax.experimental import pallas as pl
from jax.experimental.pallas import tpu as pltpu
from jax.sharding import PartitionSpec as P

EPSILON = 1e-05
MESH = pl.DeviceIdType.MESH
F32, BF16 = jnp.float32, jnp.bfloat16

Y_RING, Z_RING = 4, 8
TOK = 512
LW = 160
DM = LW * 2 * Z_RING
FS = 320
PA = 128
PB = FS - PA
MAIN, TAIL = 384, 48
GU = 2 * MAIN + 128
DN = 512
PW = GU + DN
STAT = 16
OFFSETS = (1, 3, 2)


def dot(a, b):
    return lax.dot_general(a, b, (((1,), (0,)), ((), ())), preferred_element_type=F32)


def dot_t(a, b):
    return lax.dot_general(a, b, (((1,), (1,)), ((), ())), preferred_element_type=F32)


def kernel(
    x_ref, dy_ref, w_ref, gain_ref,
    dx_ref, out_ref, gg_ref,
    x_all, dy_all, n_all, w_all, w_t, dy_loc, gu, fac, hid, act, scale, stat,
    zs, zr, xls, xlr, gsx, grx, gsy, gry, g2y, r2y, g2x, r2x, own_b, own_a, ggs, ggr,
    xs_sem, xr_sem, ts_sem, tr_sem, ws_sem, wr_sem, zs_sem, zr_sem, gs_sem, gr_sem, hs_sem, hr_sem, cs_sem, cr_sem, go_sem,
):
    s = lax.axis_index("section")
    f = lax.axis_index("fsdp")
    t = lax.axis_index("tp")
    y, h = lax.div(f, 2), lax.rem(f, 2)
    z, l = lax.div(t, 2), lax.rem(t, 2)

    def at_y(off, other=False):
        return lax.rem(y + off, Y_RING) * 2 + (1 - h if other else h)

    def at_z(off, other=False):
        return lax.rem(z + off + Z_RING, Z_RING) * 2 + (1 - l if other else l)

    y_dev = [{"fsdp": at_y(o)} for o in OFFSETS]
    x_dev = {"fsdp": at_y(0, True)}
    up_dev, down_dev = {"tp": at_z(1)}, {"tp": at_z(-1)}
    l_dev = {"tp": at_z(0, True)}
    core_dev = {"section": 1 - s}

    barrier = pltpu.get_barrier_semaphore()
    peers = y_dev + [x_dev, up_dev, down_dev, l_dev, core_dev]
    for peer in peers:
        pl.semaphore_signal(barrier, inc=1, device_id=peer, device_id_type=MESH)
    pl.semaphore_wait(barrier, len(peers))

    def copy(src, dst, send, recv, i, device):
        return pltpu.make_async_remote_copy(
            src_ref=src, dst_ref=dst, send_sem=send.at[i], recv_sem=recv.at[i],
            device_id=device, device_id_type=MESH,
        )

    def t_rows(index):
        return pl.ds(pl.multiple_of(index * LW, 32), LW)

    def f_rows(index, start=0, size=FS):
        return pl.ds(pl.multiple_of(index * FS + start, 64), size)

    class Ring:
        def __init__(self, own, whole, send, recv):
            self.own, self.whole, self.send, self.recv = own, whole, send, recv

        def sends(self, way, k, j):
            return k < 3 or j == (0 if way > 0 else 1)

        def out(self, way, k, j):
            rows = t_rows(at_z(-way * k, j == 1))
            src = self.own if k == 0 and j == 0 else self.whole.at[rows]
            i = (0 if way > 0 else 8) + 2 * k + j
            return copy(src, self.whole.at[rows], self.send, self.recv, i, up_dev if way > 0 else down_dev)

        def into(self, way, k, j):
            rows = t_rows(at_z(-way * (k + 1), j == 1))
            i = (0 if way > 0 else 8) + 2 * k + j
            return copy(self.whole.at[rows], self.whole.at[rows], self.send, self.recv, i, up_dev if way > 0 else down_dev)

        def pair(self, incoming=False):
            rows = t_rows(at_z(0, incoming))
            src = self.whole.at[rows] if incoming else self.own
            return copy(src, self.whole.at[rows], self.send, self.recv, 16, l_dev)

        def begin(self):
            self.out(1, 0, 0).start()
            self.out(-1, 0, 0).start()
            self.pair().start()
            self.whole[t_rows(t), :] = self.own[...]

        def paired(self):
            self.pair(True).wait_recv()
            self.out(1, 0, 1).start()
            self.out(-1, 0, 1).start()

        def step(self, k):
            for j in (0, 1):
                for way in (1, -1):
                    if self.sends(way, k, j):
                        self.into(way, k, j).wait_recv()
                        if k < 3 and self.sends(way, k + 1, j):
                            self.out(way, k + 1, j).start()

        def drain(self):
            for k in range(4):
                for j in (0, 1):
                    for way in (1, -1):
                        if self.sends(way, k, j):
                            self.out(way, k, j).wait_send()
            self.pair().wait_send()

    ring_x = Ring(x_ref, x_all, xs_sem, xr_sem)
    ring_t = Ring(dy_ref, dy_all, ts_sem, tr_sem)
    ring_d = Ring(dy_loc, dy_all, ts_sem, tr_sem)

    def w_copy(rows, i, device, src=None):
        block = w_all.at[rows]
        return copy(block if src is None else src, block, ws_sem, wr_sem, i, device)

    def w_full(d):
        return w_copy(f_rows(f), d, y_dev[d], w_ref)

    def w_full_in(d):
        return w_copy(f_rows(at_y(4 - OFFSETS[d])), d, y_dev[d])

    def w_a(d):
        return w_copy(f_rows(at_y(0, True), 0, PA), 3 + d, y_dev[d])

    def w_a_in(d):
        return w_copy(f_rows(at_y(4 - OFFSETS[d], True), 0, PA), 3 + d, y_dev[d])

    def w_x():
        return w_copy(f_rows(f), 6, x_dev, w_ref)

    def w_x_in():
        return w_copy(f_rows(at_y(0, True)), 6, x_dev)

    def w_b(d):
        return w_copy(f_rows(at_y(4 - OFFSETS[d]), PA, PB), 7 + d, x_dev)

    def w_b_in(d):
        return w_copy(f_rows(at_y(4 - OFFSETS[d], True), PA, PB), 7 + d, x_dev)

    def w_begin():
        w_x().start()
        for d in range(3):
            w_full(d).start()
        w_all[f_rows(f), :] = w_ref[...]

    def w_middle():
        w_x_in().wait_recv()
        for d in range(3):
            w_a(d).start()
        for d in (0, 1):
            w_full_in(d).wait_recv()
            w_b(d).start()

    def w_late():
        w_full_in(2).wait_recv()
        w_b(2).start()

    def w_end():
        for d in range(3):
            w_a_in(d).wait_recv()
            w_b_in(d).wait_recv()

    def w_drain():
        w_x().wait_send()
        for d in range(3):
            w_full(d).wait_send()
            w_a(d).wait_send()
            w_b(d).wait_send()

    @pl.when(s == 1)
    def _():
        ring_x.begin()
        w_begin()
        ring_t.begin()
        ring_x.paired()
        ring_t.paired()
        ring_x.step(0)
        ring_t.step(0)
        w_middle()
        for k in (1, 2):
            ring_x.step(k)
            ring_t.step(k)
        w_late()
        ring_x.step(3)
        ring_t.step(3)
        w_end()
        pl.semaphore_signal(go_sem, inc=1, device_id=core_dev, device_id_type=MESH)
        dy_loc[...] = dy_ref[...]
        ring_t.drain()

    @pl.when(s == 0)
    def _():
        pl.semaphore_wait(go_sem, 1)
        ring_x.begin()
        w_begin()
        ring_x.paired()
        for k in (0, 1, 2):
            ring_x.step(k)
        w_middle()
        ring_x.step(3)
        w_late()
        w_end()

    def wide(narrow):
        return jnp.concatenate([narrow] * (TOK // 128), axis=1)

    def square(i, total):
        block = x_all[t_rows(i), :].astype(F32)
        return total + jnp.sum(block * block, axis=0, keepdims=True)

    total = lax.fori_loop(0, 16, square, jnp.zeros((1, TOK), F32))
    scale[...] = lax.rsqrt(total / DM + EPSILON)

    @pl.loop(0, 16)
    def _(i):
        rows = t_rows(i)
        unit = x_all[rows, :].astype(F32) * scale[...]
        n_all[rows, :] = (unit * wide(gain_ref[rows, :])).astype(BF16)

    @pl.loop(0, PW // 128)
    def _(i):
        lanes = pl.ds(pl.multiple_of(i * 128, 128), 128)
        for k in range(Y_RING):
            w_t[lanes, 640 * k : 640 * (k + 1)] = w_all[640 * k : 640 * (k + 1), lanes].T

    @pl.loop(0, 2)
    def _(i):
        rows = pl.ds(pl.multiple_of(i * (GU // 2), 64), GU // 2)
        gu[rows, :] = dot(w_t[rows, :], n_all[...])

    spans = ((0, MAIN, MAIN, 0), (2 * MAIN, 2 * MAIN + TAIL, TAIL, MAIN))

    def factors(gate_at, up_at, size, at):
        gate, up = gu[gate_at : gate_at + size, :], gu[up_at : up_at + size, :]
        sig = jax.nn.sigmoid(gate)
        silu = gate * sig
        hid[at : at + size, :] = (silu * up).astype(BF16)
        fac[gate_at : gate_at + size, :] = up * sig * (1.0 + gate * (1.0 - sig))
        fac[up_at : up_at + size, :] = silu

    for span in spans:
        factors(*span)
    hid[MAIN + TAIL :, :] = jnp.zeros((DN - MAIN - TAIL, TOK), BF16)
    act[GU - 32 :, :] = jnp.zeros((32, TOK), BF16)

    handed = copy(dx_ref, dy_loc, cs_sem, cr_sem, 0, core_dev)

    @pl.when(s == 0)
    def _():
        handed.wait_recv()
        ring_d.begin()
        ring_d.paired()
        for k in range(4):
            ring_d.step(k)
        ring_d.drain()

    d_hid = dot(w_t[GU:, :], dy_all[...])

    def back(gate_at, up_at, size, at):
        grad = d_hid[at : at + size, :]
        d_gate = (grad * fac[gate_at : gate_at + size, :]).astype(BF16)
        d_up = (grad * fac[up_at : up_at + size, :]).astype(BF16)
        act[gate_at : gate_at + size, :] = d_gate
        act[up_at : up_at + size, :] = d_up
        return jnp.sum(
            d_gate.astype(F32) * gu[gate_at : gate_at + size, :]
            + d_up.astype(F32) * gu[up_at : up_at + size, :],
            axis=0, keepdims=True,
        )

    stat[...] = back(*spans[0]) + back(*spans[1])

    def partial(off, j):
        rows = t_rows(at_z(off, j == 1))
        return dot(w_all[rows, :GU], act[...])

    row_id = lax.broadcasted_iota(jnp.int32, (STAT, TOK), 0)

    def stat_rows(value):
        high = value.astype(BF16).astype(F32)
        low = value - high
        return jnp.where(row_id == 0, high, jnp.where(row_id == 1, low, 0.0)).astype(BF16)

    def stat_of(block):
        rows = block.astype(F32)
        return rows[0:1, :] + rows[1:2, :]

    def z_has(way, k, j):
        return k > 0 or j == (0 if way > 0 else 1)

    def z_at(way, k, j):
        return (0 if way > 0 else 8) + 2 * k + j

    def z_copy(way, k, j):
        i = z_at(way, k, j)
        size = LW + STAT if j == 0 else LW
        return copy(zs.at[i, pl.ds(0, size)], zr.at[i, pl.ds(0, size)], zs_sem, zr_sem, i, up_dev if way > 0 else down_dev)

    def z_send(way, k, j, value, total):
        i = z_at(way, k, j)
        zs[i, :LW, :] = value.astype(BF16)
        if j == 0:
            zs[i, LW:, :] = stat_rows(total)
        z_copy(way, k, j).start()

    def z_recv(way, k, j):
        i = z_at(way, k, j)
        z_copy(way, k, j).wait_recv()
        total = stat_of(zr[i, LW:, :]) if j == 0 else None
        return zr[i, :LW, :].astype(F32), total

    def z_step(k):
        for j, way in ((1, 1), (0, -1), (0, 1), (1, -1)):
            if not z_has(way, k, j):
                continue
            value = partial(way * (4 - k), j)
            total = stat[...] if j == 0 else None
            if k > 0 and z_has(way, k - 1, j):
                more, more_total = z_recv(way, k - 1, j)
                value = value + more
                if j == 0:
                    total = total + more_total
            z_send(way, k, j, value, total)

    def grads(rows):
        return dot_t(n_all[rows, :], act[...]), dot_t(dy_all[rows, :], hid[...])

    def g_x(o):
        return copy(gsx.at[o], grx.at[o], gs_sem, gr_sem, o, x_dev)

    def g_y(d):
        return copy(gsy.at[d], gry.at[d], gs_sem, gr_sem, 4 + d, y_dev[d])

    def g_y2(d):
        return copy(g2y.at[d], r2y.at[d], gs_sem, gr_sem, 7 + d, y_dev[d])

    def g_x2():
        return copy(g2x, r2x, gs_sem, gr_sem, 10, x_dev)

    def put(ref, lead, value):
        ref[(*lead, slice(None), slice(0, GU))] = value[0].astype(ref.dtype)
        ref[(*lead, slice(None), slice(GU, PW))] = value[1].astype(ref.dtype)

    def grads_x(o):
        put(gsx, (o,), grads(f_rows(at_y(o, True), PA, PB)))
        g_x(o).start()

    def grads_y(d):
        put(gsy, (d, 0), grads(f_rows(at_y(OFFSETS[d]), 0, PA)))
        put(gsy, (d, 1), grads(f_rows(at_y(OFFSETS[d], True), 0, PA)))
        g_y(d).start()

    z_step(0)
    z_step(1)
    grads_x(1)
    grads_x(3)
    z_step(2)
    grads_x(2)
    grads_x(0)
    z_step(3)
    grads_y(0)
    grads_y(1)
    sums = []
    for j in (1, 0):
        value = partial(0, j)
        total = stat[...]
        for way in (1, -1):
            more, more_total = z_recv(way, 3, j)
            value = value + more
            if j == 0:
                total = total + more_total
        sums.append((value, total))
        if j == 1:
            xls[:LW, :] = value.astype(BF16)
    d_norm, ring_total = sums[1]
    xls[LW:, :] = stat_rows(ring_total)
    to_pair = copy(xls, xlr, zs_sem, zr_sem, 16, l_dev)
    to_pair.start()
    grads_y(2)
    to_pair.wait_recv()
    d_norm = d_norm + xlr[:LW, :].astype(F32)
    norm_stat = (ring_total + stat_of(xlr[LW:, :])) / DM
    mine = t_rows(t)
    unit = x_all[mine, :].astype(F32) * scale[...]
    dx_ref[...] = (
        dy_loc[...].astype(F32)
        + scale[...] * (d_norm * wide(gain_ref[mine, :]) - unit * norm_stat)
    ).astype(BF16)

    @pl.when(s == 1)
    def _():
        handed.start()

    terms = d_norm * unit
    lanes = terms[:, :128] + terms[:, 128:256] + terms[:, 256:384] + terms[:, 384:]
    ggs[0] = lax.dot_general(
        jnp.ones((8, 128), F32), lanes, (((1,), (1,)), ((), ())),
        preferred_element_type=F32, precision=lax.Precision.HIGHEST,
    )
    gain_x = copy(ggs.at[0], ggr.at[0], hs_sem, hr_sem, 0, x_dev)
    gain_x.start()

    @pl.loop(0, Y_RING)
    def _(o):
        put(own_b, (o,), grads(f_rows(at_y(o), PA, PB)))

    put(own_a, (0,), grads(f_rows(f, 0, PA)))
    put(own_a, (1,), grads(f_rows(at_y(0, True), 0, PA)))

    gain_x.wait_recv()
    ggs[1] = ggs[0] + ggr[0]
    gain_y = [copy(ggs.at[1], ggr.at[1 + d], hs_sem, hr_sem, 1 + d, y_dev[d]) for d in range(3)]
    for d in range(3):
        gain_y[d].start()

    for d in (0, 1, 2):
        o = OFFSETS[d]
        g_x(o).wait_recv()
        g2y[d] = (own_b[o] + grx[o].astype(F32)).astype(BF16)
        g_y2(d).start()
    for d in range(3):
        g_y(d).wait_recv()
    g2x[...] = (
        own_a[1] + gry[0, 1].astype(F32) + gry[1, 1].astype(F32) + gry[2, 1].astype(F32)
    ).astype(BF16)
    g_x2().start()
    g_x(0).wait_recv()
    g_x2().wait_recv()
    out_ref[:PA, :] = (
        own_a[0] + gry[0, 0].astype(F32) + gry[1, 0].astype(F32) + gry[2, 0].astype(F32) + r2x[...].astype(F32)
    )
    for d in range(3):
        gain_y[d].wait_recv()
    gg_ref[...] = ggs[1] + ggr[1] + ggr[2] + ggr[3]
    for d in range(3):
        g_y2(d).wait_recv()
    out_ref[PA:, :] = (
        own_b[0] + grx[0].astype(F32) + r2y[0].astype(F32) + r2y[1].astype(F32) + r2y[2].astype(F32)
    )

    ring_x.drain()
    w_drain()
    for k in range(4):
        for j in (0, 1):
            for way in (1, -1):
                if z_has(way, k, j):
                    z_copy(way, k, j).wait_send()
    to_pair.wait_send()
    for o in range(4):
        g_x(o).wait_send()
    for d in range(3):
        g_y(d).wait_send()
        g_y2(d).wait_send()
        gain_y[d].wait_send()
    g_x2().wait_send()
    gain_x.wait_send()

    @pl.when(s == 1)
    def _():
        handed.wait_send()


def window(x_t, dy_t, w, gain):
    vmem = pl.BlockSpec(memory_space=pltpu.VMEM)
    dma = pltpu.SemaphoreType.DMA
    return pl.pallas_call(
        kernel,
        name="window",
        out_shape=(
            jax.ShapeDtypeStruct((LW, TOK), BF16),
            jax.ShapeDtypeStruct((FS, PW), F32),
            jax.ShapeDtypeStruct((8, LW), F32),
        ),
        in_specs=[vmem] * 4,
        out_specs=(vmem,) * 3,
        scratch_shapes=[
            pltpu.VMEM((DM, TOK), BF16),
            pltpu.VMEM((DM, TOK), BF16),
            pltpu.VMEM((DM, TOK), BF16),
            pltpu.VMEM((DM, PW), BF16),
            pltpu.VMEM((PW, DM), BF16),
            pltpu.VMEM((LW, TOK), BF16),
            pltpu.VMEM((GU, TOK), F32),
            pltpu.VMEM((GU, TOK), F32),
            pltpu.VMEM((DN, TOK), BF16),
            pltpu.VMEM((GU, TOK), BF16),
            pltpu.VMEM((1, TOK), F32),
            pltpu.VMEM((1, TOK), F32),
            pltpu.VMEM((16, LW + STAT, TOK), BF16),
            pltpu.VMEM((16, LW + STAT, TOK), BF16),
            pltpu.VMEM((LW + STAT, TOK), BF16),
            pltpu.VMEM((LW + STAT, TOK), BF16),
            pltpu.VMEM((4, PB, PW), BF16),
            pltpu.VMEM((4, PB, PW), BF16),
            pltpu.VMEM((3, 2, PA, PW), BF16),
            pltpu.VMEM((3, 2, PA, PW), BF16),
            pltpu.VMEM((3, PB, PW), BF16),
            pltpu.VMEM((3, PB, PW), BF16),
            pltpu.VMEM((PA, PW), BF16),
            pltpu.VMEM((PA, PW), BF16),
            pltpu.VMEM((4, PB, PW), F32),
            pltpu.VMEM((2, PA, PW), F32),
            pltpu.VMEM((2, 8, LW), F32),
            pltpu.VMEM((4, 8, LW), F32),
            dma((17,)), dma((17,)), dma((17,)), dma((17,)), dma((10,)), dma((10,)),
            dma((17,)), dma((17,)), dma((11,)), dma((11,)), dma((4,)), dma((4,)), dma((1,)), dma((1,)),
            pltpu.SemaphoreType.REGULAR,
        ],
        compiler_params=pltpu.CompilerParams(
            collective_id=0, has_side_effects=True, vmem_limit_bytes=67043328
        ),
    )(x_t, dy_t, w, gain)


def shards(saved_inputs, top_grad, norm_gain, gate_weight, up_weight, down_weight):
    micro, rows, width = saved_inputs.shape[1:]
    x_t = saved_inputs[0].reshape(micro * rows, width).T
    dy_t = top_grad.reshape(micro * rows, width).T
    gate, up, down = gate_weight[0], up_weight[0], down_weight[0].T
    blank = functools.partial(jnp.zeros, dtype=BF16)
    packed = jnp.concatenate(
        [gate[:, :MAIN], up[:, :MAIN], gate[:, MAIN:], up[:, MAIN:], blank((FS, 128 - 2 * TAIL)),
         down, blank((FS, DN - MAIN - TAIL))], axis=1,
    )
    gain = jnp.broadcast_to(norm_gain[0][:, None], (DM, 128))
    dx, grad, gain_grad = window(x_t, dy_t, packed, gain)
    gate_grad = jnp.concatenate([grad[:, :MAIN], grad[:, 2 * MAIN : 2 * MAIN + TAIL]], axis=1)
    up_grad = jnp.concatenate([grad[:, MAIN : 2 * MAIN], grad[:, 2 * MAIN + TAIL : 2 * MAIN + 2 * TAIL]], axis=1)
    down_grad = grad[:, GU : GU + MAIN + TAIL].T
    dx = dx.T.reshape(micro, rows, width)
    return (dx[None], gate_grad[None], up_grad[None], down_grad[None], gain_grad[:1])


def solution(mesh):
    placed = (
        P("section", None, "fsdp", "tp"),
        P(None, "fsdp", "tp"),
        P("section", None),
        P("section", "fsdp", "tp"),
        P("section", "fsdp", "tp"),
        P("section", "tp", "fsdp"),
    )
    return jax.shard_map(
        shards,
        mesh=mesh,
        in_specs=placed,
        out_specs=(
            P("section", None, "fsdp", "tp"),
            P("section", "fsdp", "tp"),
            P("section", "fsdp", "tp"),
            P("section", "tp", "fsdp"),
            P("section", "tp"),
        ),
        check_vma=False,
    )
```

profile of v0, /device:TPU:8, one launch (start us, length us, event | category | flops | bytes accessed | tf_op | source)
XLA Modules:
  0.0 217.8 jit_solution(3379407938241223528)
XLA Ops:
  0.6 0.0 copy-start.1
  0.6 0.0 copy-start.2
  0.7 0.8 reduce
  1.5 0.9 slice.42
  2.3 0.9 slice.43
  3.2 1.7 copy.17
  5.0 1.7 copy.18
  6.7 1.0 slice.40
  7.7 0.0 copy-done.2
  7.8 0.0 copy-done.1
  7.8 1.2 concatenate.9.w_ref
  8.9 1.5 broadcast_in_dim.25.gain_ref
  10.4 199.9 %window.1 = (bf16[160,512]{1,0:T(8,128)(2,1)}, f32[320,1408]{1,0:T(8,128)}, f32[8,160]{1,0:T(8,128)}) custom-call(bf16[160,512]{1,0:T(8,128)(2,1)} %bitcast.19, bf16[160,512]{1,0:T(8,128)(2,1)} %bitcast.20, bf16[320,1408]{1,0:T(8,128)(2,1)} %concatenate.9.w_ref, f32[2560,128]{1,0:T(8,128)} %broadcast_in_dim.25.gain_ref), custom_call_target="tpu_custom_call" | custom-call | tf_op jit(solution)/shard_map/window/pallas_call | solution.py:488
  210.3 0.0 copy-start
  210.3 1.4 slice.39
  211.7 1.8 copy.19
  213.5 1.1 fusion.1
  214.6 2.0 slice_bitcast_fusion
  216.5 0.0 copy-done
  216.5 0.1 fusion
  216.6 1.2 maximum_bitcast_fusion
  (3 shorter events, 0.1 us)
Async XLA Ops:
  0.6 7.1 %copy-start.1 = (bf16[1,432,320]{1,2,0:T(8,128)(2,1)S(1)}, bf16[1,432,320]{1,2,0:T(8,128)(2,1)}, u32[]{:S(2)}) copy-start(bf16[1,432,320]{1,2,0:T(8,128)(2,1)} %param.11) | copy-start | bytes 829444
  0.6 7.0 %copy-start.2 = (bf16[1,320,432]{2,1,0:T(8,128)(2,1)S(1)}, bf16[1,320,432]{2,1,0:T(8,128)(2,1)}, u32[]{:S(2)}) copy-start(bf16[1,320,432]{2,1,0:T(8,128)(2,1)} %param.10) | copy-start | bytes 829444
  210.3 6.2 %copy-start = (f32[320,1408]{1,0:T(8,128)S(1)}, f32[320,1408]{1,0:T(8,128)}, u32[]{:S(2)}) copy-start(f32[320,1408]{1,0:T(8,128)} %get-tuple-element.9) | copy-start | bytes 5406724
where the time goes:
time: 218 us
  Pallas kernels  200 us (92%)
  local copies, waits for them, and re-layouts  15.2 us (7%)
    pallas_call x1, Pallas kernels, window(): pl.pallas_call(kernel, name='window', out_shape=(jax.ShapeDtypeStruct((LW...  200 us

commit v1 on v0

v1 whole, which is shorter than its diff:
```python
import jax
import jax.numpy as jnp
from jax import lax
from jax.experimental import pallas as pl
from jax.experimental.pallas import tpu as pltpu
from jax.sharding import PartitionSpec as P

EPSILON = 1e-05
MESH = pl.DeviceIdType.MESH
F32, BF16 = jnp.float32, jnp.bfloat16

Y_RING, Z_RING = 4, 8
TOK = 512
LW = 160
DM = LW * 2 * Z_RING
FS = 320
PA = 144
PB = FS - PA
MAIN, TAIL = 384, 48
GU = 2 * MAIN + 128
DN = 512
PW = GU + DN
STAT = 16
PIECES = 2
PR = LW // PIECES
OFFSETS = (1, 3, 2)


def dot(a, b):
    return lax.dot_general(a, b, (((1,), (0,)), ((), ())), preferred_element_type=F32)


def dot_t(a, b):
    return lax.dot_general(a, b, (((1,), (1,)), ((), ())), preferred_element_type=F32)


def kernel(
    x_ref, dy_ref, gain_ref, gate_ref, up_ref, down_ref,
    dx_ref, gate_grad, up_grad, down_grad, gain_grad,
    x_all, dy_all, n_all, w_all, w_t, dy_loc, dx_t, gain_col, gu, fac, hid, act, scale, stat,
    zs, zr, xls, xlr, gsx, grx, gsy, gry, g2y, r2y, g2x, r2x, own_b, own_a, ggs, ggr,
    xs_sem, xr_sem, ts_sem, tr_sem, ws_sem, wr_sem, zs_sem, zr_sem, gs_sem, gr_sem, hs_sem, hr_sem, cs_sem, cr_sem, go_sem,
):
    s = lax.axis_index("section")
    f = lax.axis_index("fsdp")
    t = lax.axis_index("tp")
    y, h = lax.div(f, 2), lax.rem(f, 2)
    z, l = lax.div(t, 2), lax.rem(t, 2)

    def at_y(off, other=False):
        return lax.rem(y + off, Y_RING) * 2 + (1 - h if other else h)

    def at_z(off, other=False):
        return lax.rem(z + off + Z_RING, Z_RING) * 2 + (1 - l if other else l)

    y_dev = [{"fsdp": at_y(o)} for o in OFFSETS]
    x_dev = {"fsdp": at_y(0, True)}
    up_dev, down_dev = {"tp": at_z(1)}, {"tp": at_z(-1)}
    l_dev = {"tp": at_z(0, True)}
    core_dev = {"section": 1 - s}

    def t_rows(index, start=0, size=LW):
        return pl.ds(pl.multiple_of(index * LW + start, 16), size)

    def f_rows(index, start=0, size=FS):
        return pl.ds(pl.multiple_of(index * FS + start, 16), size)

    far_dev = [{"fsdp": at_y(o, True)} for o in OFFSETS]
    f_devs = y_dev + [x_dev] + far_dev
    barrier = pltpu.get_barrier_semaphore()
    peers = f_devs + [up_dev, down_dev, l_dev, core_dev]
    for peer in peers:
        pl.semaphore_signal(barrier, inc=1, device_id=peer, device_id_type=MESH)

    x_all[t_rows(t), :] = x_ref[...].T

    @pl.when(s == 1)
    def _():
        block = dy_ref[...].T
        dy_all[t_rows(t), :] = block
        dy_loc[...] = block

    mine_w = f_rows(f)
    w_all[mine_w, 0:MAIN] = gate_ref[:, 0:MAIN]
    w_all[mine_w, MAIN : 2 * MAIN] = up_ref[:, 0:MAIN]
    w_all[mine_w, 2 * MAIN : GU] = jnp.concatenate(
        [gate_ref[:, MAIN:], up_ref[:, MAIN:], jnp.zeros((FS, 128 - 2 * TAIL), BF16)], axis=1
    )
    w_all[mine_w, GU : GU + MAIN] = down_ref[:, 0:MAIN]
    w_all[mine_w, GU + MAIN : PW] = jnp.concatenate(
        [down_ref[:, MAIN:], jnp.zeros((FS, 128 - TAIL), BF16)], axis=1
    )
    pl.semaphore_wait(barrier, len(peers))

    def copy(src, dst, send, recv, i, device):
        return pltpu.make_async_remote_copy(
            src_ref=src, dst_ref=dst, send_sem=send.at[i], recv_sem=recv.at[i],
            device_id=device, device_id_type=MESH,
        )

    class Ring:
        def __init__(self, whole, send, recv):
            self.whole, self.send, self.recv = whole, send, recv

        def sends(self, way, k, j):
            return k < 3 or j == (0 if way > 0 else 1)

        def piece(self, index, i, q, device):
            block = self.whole.at[t_rows(index, q * PR, PR)]
            return copy(block, block, self.send, self.recv, i * PIECES + q, device)

        def out(self, way, k, j, q):
            i = (0 if way > 0 else 8) + 2 * k + j
            return self.piece(at_z(-way * k, j == 1), i, q, up_dev if way > 0 else down_dev)

        def into(self, way, k, j, q):
            i = (0 if way > 0 else 8) + 2 * k + j
            return self.piece(at_z(-way * (k + 1), j == 1), i, q, up_dev if way > 0 else down_dev)

        def pair(self, q, incoming=False):
            return self.piece(at_z(0, incoming), 16, q, l_dev)

        def begin(self):
            for q in range(PIECES):
                self.pair(q).start()
                self.out(1, 0, 0, q).start()
                self.out(-1, 0, 0, q).start()

        def paired(self):
            for q in range(PIECES):
                self.pair(q, True).wait_recv()
                self.out(1, 0, 1, q).start()
                self.out(-1, 0, 1, q).start()

        def step(self, k):
            for j in (0, 1):
                for q in range(PIECES):
                    for way in (1, -1):
                        if self.sends(way, k, j):
                            self.into(way, k, j, q).wait_recv()
                            if k < 3 and self.sends(way, k + 1, j):
                                self.out(way, k + 1, j, q).start()

        def drain(self):
            for q in range(PIECES):
                for k in range(4):
                    for j in (0, 1):
                        for way in (1, -1):
                            if self.sends(way, k, j):
                                self.out(way, k, j, q).wait_send()
                self.pair(q).wait_send()

    ring_x = Ring(x_all, xs_sem, xr_sem)
    ring_t = Ring(dy_all, ts_sem, tr_sem)

    def w_copy(rows, i, device):
        return copy(w_all.at[rows], w_all.at[rows], ws_sem, wr_sem, i, device)

    def w_full(d):
        return w_copy(f_rows(f), d, y_dev[d])

    def w_full_in(d):
        return w_copy(f_rows(at_y(4 - OFFSETS[d])), d, y_dev[d])

    def w_a(d):
        return w_copy(f_rows(at_y(0, True), 0, PA), 3 + d, y_dev[d])

    def w_a_in(d):
        return w_copy(f_rows(at_y(4 - OFFSETS[d], True), 0, PA), 3 + d, y_dev[d])

    def w_x():
        return w_copy(f_rows(f), 6, x_dev)

    def w_x_in():
        return w_copy(f_rows(at_y(0, True)), 6, x_dev)

    def w_b(d):
        return w_copy(f_rows(at_y(4 - OFFSETS[d]), PA, PB), 7 + d, x_dev)

    def w_b_in(d):
        return w_copy(f_rows(at_y(4 - OFFSETS[d], True), PA, PB), 7 + d, x_dev)

    def w_begin():
        w_x().start()
        for d in range(3):
            w_full(d).start()

    def w_middle():
        w_x_in().wait_recv()
        for d in range(3):
            w_a(d).start()
        for d in (0, 1):
            w_full_in(d).wait_recv()
            w_b(d).start()

    def w_late():
        w_full_in(2).wait_recv()
        w_b(2).start()

    def w_end():
        for d in range(3):
            w_a_in(d).wait_recv()
            w_b_in(d).wait_recv()

    def w_drain():
        w_x().wait_send()
        for d in range(3):
            w_full(d).wait_send()
            w_a(d).wait_send()
            w_b(d).wait_send()

    def columns():
        @pl.loop(0, DM // 128)
        def _(i):
            lanes = pl.ds(pl.multiple_of(i * 128, 128), 128)
            gain_col[lanes, :] = jnp.broadcast_to(gain_ref[:, lanes], (128, 128)).T

    @pl.when(s == 0)
    def _():
        columns()

    @pl.when(s == 1)
    def _():
        ring_x.begin()
        ring_t.begin()
        w_begin()
        columns()
        ring_x.paired()
        ring_t.paired()
        ring_x.step(0)
        ring_t.step(0)
        w_middle()
        ring_x.step(1)
        ring_t.step(1)
        ring_x.step(2)
        w_late()
        ring_t.step(2)
        ring_x.step(3)
        ring_t.step(3)
        pl.semaphore_signal(go_sem.at[0], inc=1, device_id=core_dev, device_id_type=MESH)

    @pl.when(s == 0)
    def _():
        pl.semaphore_wait(go_sem.at[0], 1)
        ring_x.begin()
        ring_x.paired()
        ring_x.step(0)
        pl.semaphore_wait(go_sem.at[1], 1)
        w_begin()
        for k in (1, 2, 3):
            ring_x.step(k)
        w_middle()
        w_late()

    def wide(narrow):
        return jnp.concatenate([narrow] * (TOK // 128), axis=1)

    def square(i, total):
        block = x_all[t_rows(i), :].astype(F32)
        return total + jnp.sum(block * block, axis=0, keepdims=True)

    total = lax.fori_loop(0, 16, square, jnp.zeros((1, TOK), F32))
    scale[...] = lax.rsqrt(total / DM + EPSILON)

    @pl.loop(0, 16)
    def _(i):
        rows = t_rows(i)
        unit = x_all[rows, :].astype(F32) * scale[...]
        n_all[rows, :] = (unit * wide(gain_col[rows, :])).astype(BF16)

    w_end()

    @pl.when(s == 1)
    def _():
        pl.semaphore_signal(go_sem.at[1], inc=1, device_id=core_dev, device_id_type=MESH)

    @pl.loop(0, PW // 128)
    def _(i):
        lanes = pl.ds(pl.multiple_of(i * 128, 128), 128)
        for k in range(Y_RING):
            w_t[lanes, 640 * k : 640 * (k + 1)] = w_all[640 * k : 640 * (k + 1), lanes].T

    @pl.loop(0, 2)
    def _(i):
        rows = pl.ds(pl.multiple_of(i * (GU // 2), 64), GU // 2)
        gu[rows, :] = dot(w_t[rows, :], n_all[...])

    spans = ((0, MAIN, MAIN, 0), (2 * MAIN, 2 * MAIN + TAIL, TAIL, MAIN))

    def factors(gate_at, up_at, size, at):
        gate, up = gu[gate_at : gate_at + size, :], gu[up_at : up_at + size, :]
        sig = jax.nn.sigmoid(gate)
        silu = gate * sig
        hid[at : at + size, :] = (silu * up).astype(BF16)
        fac[gate_at : gate_at + size, :] = up * sig * (1.0 + gate * (1.0 - sig))
        fac[up_at : up_at + size, :] = silu

    for span in spans:
        factors(*span)
    hid[MAIN + TAIL :, :] = jnp.zeros((DN - MAIN - TAIL, TOK), BF16)
    act[GU - 32 :, :] = jnp.zeros((32, TOK), BF16)

    handed = copy(dx_t, dy_loc, cs_sem, cr_sem, 0, core_dev)

    @pl.when(s == 0)
    def _():
        handed.wait_recv()
        dy_all[t_rows(t), :] = dy_loc[...]
        ring_t.begin()
        ring_t.paired()
        for k in range(4):
            ring_t.step(k)

    d_hid = dot(w_t[GU:, :], dy_all[...])

    def back(gate_at, up_at, size, at):
        grad = d_hid[at : at + size, :]
        d_gate = (grad * fac[gate_at : gate_at + size, :]).astype(BF16)
        d_up = (grad * fac[up_at : up_at + size, :]).astype(BF16)
        act[gate_at : gate_at + size, :] = d_gate
        act[up_at : up_at + size, :] = d_up
        return jnp.sum(
            d_gate.astype(F32) * gu[gate_at : gate_at + size, :]
            + d_up.astype(F32) * gu[up_at : up_at + size, :],
            axis=0, keepdims=True,
        )

    stat[...] = back(*spans[0]) + back(*spans[1])

    def partial(off, j):
        rows = t_rows(at_z(off, j == 1))
        return dot(w_all[rows, :GU], act[...])

    row_id = lax.broadcasted_iota(jnp.int32, (STAT, TOK), 0)

    def stat_rows(value):
        high = value.astype(BF16).astype(F32)
        low = value - high
        return jnp.where(row_id == 0, high, jnp.where(row_id == 1, low, 0.0)).astype(BF16)

    def stat_of(block):
        rows = block.astype(F32)
        return rows[0:1, :] + rows[1:2, :]

    def z_has(way, k, j):
        return k > 0 or j == (0 if way > 0 else 1)

    def z_at(way, k, j):
        return (0 if way > 0 else 8) + 2 * k + j

    def z_rows(j, q):
        extra = STAT if j == 0 and q == PIECES - 1 else 0
        return slice(q * PR, (q + 1) * PR + extra)

    def z_copy(way, k, j, q):
        i, rows = z_at(way, k, j), z_rows(j, q)
        part = pl.ds(rows.start, rows.stop - rows.start)
        return copy(zs.at[i, part], zr.at[i, part], zs_sem, zr_sem, i * PIECES + q, up_dev if way > 0 else down_dev)

    def z_step(k):
        for j, way in ((1, 1), (0, -1), (0, 1), (1, -1)):
            if not z_has(way, k, j):
                continue
            value = partial(way * (4 - k), j)
            i, more = z_at(way, k, j), z_at(way, k - 1, j)
            adds = k > 0 and z_has(way, k - 1, j)
            for q in range(PIECES):
                rows = slice(q * PR, (q + 1) * PR)
                part = value[rows, :]
                if adds:
                    z_copy(way, k - 1, j, q).wait_recv()
                    part = part + zr[more, rows, :].astype(F32)
                zs[i, rows, :] = part.astype(BF16)
                if j == 0 and q == PIECES - 1:
                    total = stat[...]
                    if adds:
                        total = total + stat_of(zr[more, LW:, :])
                    zs[i, LW:, :] = stat_rows(total)
                z_copy(way, k, j, q).start()

    to_pair = copy(xls, xlr, zs_sem, zr_sem, 16 * PIECES, l_dev)

    def z_end():
        for j in (1, 0):
            value = partial(0, j)
            total = stat[...]
            for way in (1, -1):
                i = z_at(way, 3, j)
                for q in range(PIECES):
                    z_copy(way, 3, j, q).wait_recv()
                value = value + zr[i, :LW, :].astype(F32)
                if j == 0:
                    total = total + stat_of(zr[i, LW:, :])
            if j == 1:
                xls[:LW, :] = value.astype(BF16)
        xls[LW:, :] = stat_rows(total)
        to_pair.start()
        return value, total

    def finish(value, total):
        to_pair.wait_recv()
        d_norm = value + xlr[:LW, :].astype(F32)
        norm_stat = (total + stat_of(xlr[LW:, :])) / DM
        mine = t_rows(t)
        unit = x_all[mine, :].astype(F32) * scale[...]
        dx_t[...] = (
            dy_loc[...].astype(F32)
            + scale[...] * (d_norm * wide(gain_col[mine, :]) - unit * norm_stat)
        ).astype(BF16)
        return d_norm * unit

    gains = [copy(ggs, ggr.at[i], hs_sem, hr_sem, i, f_devs[i]) for i in range(7)]

    def send_gain(terms):
        lanes = terms[:, :128] + terms[:, 128:256] + terms[:, 256:384] + terms[:, 384:]
        ggs[...] = lax.dot_general(
            jnp.ones((8, 128), F32), lanes, (((1,), (1,)), ((), ())),
            preferred_element_type=F32, precision=lax.Precision.HIGHEST,
        )
        for one in gains:
            one.start()

    def grads(rows):
        return dot_t(n_all[rows, :], act[...]), dot_t(dy_all[rows, :], hid[...])

    def g_x(o):
        return copy(gsx.at[o], grx.at[o], gs_sem, gr_sem, o, x_dev)

    def g_y(d):
        return copy(gsy.at[d], gry.at[d], gs_sem, gr_sem, 4 + d, y_dev[d])

    def g_y2(d):
        return copy(g2y.at[d], r2y.at[d], gs_sem, gr_sem, 7 + d, y_dev[d])

    def g_x2():
        return copy(g2x, r2x, gs_sem, gr_sem, 10, x_dev)

    def put(ref, lead, value):
        ref[(*lead, slice(None), slice(0, GU))] = value[0].astype(ref.dtype)
        ref[(*lead, slice(None), slice(GU, PW))] = value[1].astype(ref.dtype)

    def grads_x(o):
        put(gsx, (o,), grads(f_rows(at_y(o, True), PA, PB)))
        g_x(o).start()

    def grads_y(d):
        put(gsy, (d, 0), grads(f_rows(at_y(OFFSETS[d]), 0, PA)))
        put(gsy, (d, 1), grads(f_rows(at_y(OFFSETS[d], True), 0, PA)))
        g_y(d).start()

    def grads_all():
        for o in (1, 3, 2, 0):
            grads_x(o)
        for d in range(3):
            grads_y(d)

        @pl.loop(0, Y_RING)
        def _(o):
            put(own_b, (o,), grads(f_rows(at_y(o), PA, PB)))

        put(own_a, (0,), grads(f_rows(f, 0, PA)))
        put(own_a, (1,), grads(f_rows(at_y(0, True), 0, PA)))

    def second_b(d):
        o = OFFSETS[d]
        g_x(o).wait_recv()
        g2y[d] = (own_b[o] + grx[o].astype(F32)).astype(BF16)
        g_y2(d).start()

    def second_a():
        for d in range(3):
            g_y(d).wait_recv()
        g2x[...] = (
            own_a[1] + gry[0, 1].astype(F32) + gry[1, 1].astype(F32) + gry[2, 1].astype(F32)
        ).astype(BF16)
        g_x2().start()

    @pl.when(s == 1)
    def _():
        for k in range(4):
            z_step(k)
        terms = finish(*z_end())
        handed.start()
        send_gain(terms)
        grads_all()
        second_b(0)
        second_b(1)
        second_a()
        second_b(2)

    @pl.when(s == 0)
    def _():
        grads_all()
        z_step(0)
        z_step(1)
        second_b(0)
        z_step(2)
        second_b(1)
        z_step(3)
        second_a()
        second_b(2)
        send_gain(finish(*z_end()))

    dx_ref[...] = dx_t[...].T

    def unpack(rows, value):
        gate_grad[rows, :MAIN] = value[:, :MAIN]
        up_grad[rows, :MAIN] = value[:, MAIN : 2 * MAIN]
        gate_grad[rows, MAIN:] = value[:, 2 * MAIN : 2 * MAIN + TAIL]
        up_grad[rows, MAIN:] = value[:, 2 * MAIN + TAIL : 2 * MAIN + 2 * TAIL]
        down_grad[rows, :] = value[:, GU : GU + MAIN + TAIL]

    g_x2().wait_recv()
    unpack(slice(0, PA), (
        own_a[0] + gry[0, 0].astype(F32) + gry[1, 0].astype(F32) + gry[2, 0].astype(F32) + r2x[...].astype(F32)
    ))
    g_x(0).wait_recv()
    for d in range(3):
        g_y2(d).wait_recv()
    unpack(slice(PA, FS), (
        own_b[0] + grx[0].astype(F32) + r2y[0].astype(F32) + r2y[1].astype(F32) + r2y[2].astype(F32)
    ))
    summed = ggs[...]
    for i in range(7):
        gains[i].wait_recv()
        summed = summed + ggr[i]
    gain_grad[...] = summed[:1, :]

    ring_x.drain()
    ring_t.drain()
    w_drain()
    for k in range(4):
        for j in (0, 1):
            for way in (1, -1):
                if z_has(way, k, j):
                    for q in range(PIECES):
                        z_copy(way, k, j, q).wait_send()
    to_pair.wait_send()
    for o in range(4):
        g_x(o).wait_send()
    for d in range(3):
        g_y(d).wait_send()
        g_y2(d).wait_send()
    g_x2().wait_send()
    for one in gains:
        one.wait_send()

    @pl.when(s == 1)
    def _():
        handed.wait_send()


def window(*args):
    vmem = pl.BlockSpec(memory_space=pltpu.VMEM)
    dma = pltpu.SemaphoreType.DMA
    ring = dma((17 * PIECES,))
    return pl.pallas_call(
        kernel,
        name="window",
        out_shape=(
            jax.ShapeDtypeStruct((TOK, LW), BF16),
            jax.ShapeDtypeStruct((FS, MAIN + TAIL), F32),
            jax.ShapeDtypeStruct((FS, MAIN + TAIL), F32),
            jax.ShapeDtypeStruct((FS, MAIN + TAIL), F32),
            jax.ShapeDtypeStruct((1, LW), F32),
        ),
        in_specs=[vmem] * 6,
        out_specs=(vmem,) * 5,
        scratch_shapes=[
            pltpu.VMEM((DM, TOK), BF16),
            pltpu.VMEM((DM, TOK), BF16),
            pltpu.VMEM((DM, TOK), BF16),
            pltpu.VMEM((DM, PW), BF16),
            pltpu.VMEM((PW, DM), BF16),
            pltpu.VMEM((LW, TOK), BF16),
            pltpu.VMEM((LW, TOK), BF16),
            pltpu.VMEM((DM, 128), F32),
            pltpu.VMEM((GU, TOK), F32),
            pltpu.VMEM((GU, TOK), F32),
            pltpu.VMEM((DN, TOK), BF16),
            pltpu.VMEM((GU, TOK), BF16),
            pltpu.VMEM((1, TOK), F32),
            pltpu.VMEM((1, TOK), F32),
            pltpu.VMEM((16, LW + STAT, TOK), BF16),
            pltpu.VMEM((16, LW + STAT, TOK), BF16),
            pltpu.VMEM((LW + STAT, TOK), BF16),
            pltpu.VMEM((LW + STAT, TOK), BF16),
            pltpu.VMEM((4, PB, PW), BF16),
            pltpu.VMEM((4, PB, PW), BF16),
            pltpu.VMEM((3, 2, PA, PW), BF16),
            pltpu.VMEM((3, 2, PA, PW), BF16),
            pltpu.VMEM((3, PB, PW), BF16),
            pltpu.VMEM((3, PB, PW), BF16),
            pltpu.VMEM((PA, PW), BF16),
            pltpu.VMEM((PA, PW), BF16),
            pltpu.VMEM((4, PB, PW), F32),
            pltpu.VMEM((2, PA, PW), F32),
            pltpu.VMEM((8, LW), F32),
            pltpu.VMEM((7, 8, LW), F32),
            ring, ring, ring, ring, dma((10,)), dma((10,)),
            ring, ring, dma((11,)), dma((11,)), dma((7,)), dma((7,)), dma((1,)), dma((1,)),
            pltpu.SemaphoreType.REGULAR((2,)),
        ],
        compiler_params=pltpu.CompilerParams(
            collective_id=0, has_side_effects=True, vmem_limit_bytes=67043328
        ),
    )(*args)


def shards(saved_inputs, top_grad, norm_gain, gate_weight, up_weight, down_weight):
    micro, rows, width = saved_inputs.shape[1:]
    dx, gate_grad, up_grad, down_grad, gain_grad = window(
        saved_inputs[0].reshape(micro * rows, width), top_grad.reshape(micro * rows, width),
        norm_gain, gate_weight[0], up_weight[0], down_weight[0].T,
    )
    return (
        dx.reshape(1, micro, rows, width), gate_grad[None], up_grad[None], down_grad.T[None], gain_grad
    )


def solution(mesh):
    placed = (
        P("section", None, "fsdp", "tp"),
        P(None, "fsdp", "tp"),
        P("section", None),
        P("section", "fsdp", "tp"),
        P("section", "fsdp", "tp"),
        P("section", "tp", "fsdp"),
    )
    return jax.shard_map(
        shards,
        mesh=mesh,
        in_specs=placed,
        out_specs=(
            P("section", None, "fsdp", "tp"),
            P("section", "fsdp", "tp"),
            P("section", "fsdp", "tp"),
            P("section", "tp", "fsdp"),
            P("section", "tp"),
        ),
        check_vma=False,
    )
```

time: 218 us -> 175 us (0.80)
  Pallas kernels: 200 us -> 167 us
  local copies, waits for them, and re-layouts: 15.2 us -> 6.43 us
    pallas_call x1, Pallas kernels: 200 us -> 167 us  [window(): pl.pallas_call(kernel, name='window', out_shape=(jax.ShapeDtypeStruct((TO...]
    slice x7 -> x0, local copies, waits for them, and re-layouts: 5.33 us -> none  [the longest x1 1.39 us: shards(): gain_grad[:1]]
    unnamed x7 -> x11, local copies, waits for them, and re-layouts: 1.77 us -> 6.43 us
    broadcast_in_dim x4 -> x0, local copies, waits for them, and re-layouts: 3.49 us -> none  [the longest x1 1.97 us: shards(): down_grad[None]]
where the time goes in v1:
time: 175 us; the launch traced here: 174 us
  Pallas kernels  167 us (95%)
  local copies, waits for them, and re-layouts  6.43 us (4%)
    pallas_call x1, Pallas kernels, window(): pl.pallas_call(kernel, name='window', out_shape=(jax.ShapeDtypeStruct((TO...  167 us
    unnamed x11, local copies, waits for them, and re-layouts  6.43 us

profile of v1, /device:TPU:8, one launch (start us, length us, event | category | flops | bytes accessed | tf_op | source)
XLA Modules:
  0.0 173.9 jit_solution(4918759432028064392)
XLA Ops:
  0.6 166.8 %window.1 = (bf16[512,160]{1,0:T(8,128)(2,1)}, f32[320,432]{1,0:T(8,128)}, f32[320,432]{1,0:T(8,128)}, f32[320,432]{1,0:T(8,128)}, f32[1,160]{1,0:T(1,128)}) custom-call(bf16[512,160]{1,0:T(8,128)(2,1)} %bitcast.20, bf16[512,160]{1,0:T(8,128)(2,1)} %bitcast.21, f32[1,2560]{1,0:T(1,128)} %gain_ref.1, bf16[320,432]{1,0:T(8,128)(2,1)} %bitcast.16, ...), custom_call_target="tpu_custom_call" | custom-call | tf_op jit(solution)/shard_map/window/pallas_call | solution.py:557
  167.4 1.7 copy.16
  169.1 0.0 copy-start.1
  169.1 2.0 %copy.17 = f32[1,320,432]{2,1,0:T(8,128)} copy(f32[1,320,432]{2,1,0:T(8,128)} %bitcast.15) | data formatting | bytes 1105920
  171.1 0.0 copy-done.1
  171.1 0.0 copy-start
  171.1 0.8 copy.18
  172.0 0.5 copy-done
  172.5 0.0 copy-start.2
  172.5 0.8 copy.19
  173.3 0.0 copy-done.2
  173.3 0.6 copy.20
Async XLA Ops:
  169.1 2.0 %copy-start.1 = (f32[320,432]{1,0:T(8,128)S(1)}, f32[320,432]{1,0:T(8,128)}, u32[]{:S(2)}) copy-start(f32[320,432]{1,0:T(8,128)} %get-tuple-element.12) | copy-start | bytes 1658884
  171.1 1.3 copy-start
  172.5 0.8 copy-start.2

commit v2 on v1

--- a/solution.py
+++ b/solution.py
@@ -14,7 +14,7 @@
 LW = 160
 DM = LW * 2 * Z_RING
 FS = 320
-PA = 144
+PA = 192
 PB = FS - PA
 MAIN, TAIL = 384, 48
 GU = 2 * MAIN + 128
@@ -23,7 +23,8 @@
 STAT = 16
 PIECES = 2
 PR = LW // PIECES
-OFFSETS = (1, 3, 2)
+WAYS = (1, -1)
+LANES = ((0, 2 * MAIN), (2 * MAIN, PW - 2 * MAIN))
 
 
 def dot(a, b):
@@ -37,8 +38,8 @@
 def kernel(
     x_ref, dy_ref, gain_ref, gate_ref, up_ref, down_ref,
     dx_ref, gate_grad, up_grad, down_grad, gain_grad,
-    x_all, dy_all, n_all, w_all, w_t, dy_loc, dx_t, gain_col, gu, fac, hid, act, scale, stat,
-    zs, zr, xls, xlr, gsx, grx, gsy, gry, g2y, r2y, g2x, r2x, own_b, own_a, ggs, ggr,
+    x_all, dy_all, n_all, w_all, w_t, dx_t, gain_col, gu, fac, hid, act, scale, stat,
+    zs, zr, xls, xlr, ahs, ahr, afs, afr, bxs, bxr, bhs, bhr, bfs, bfr, axs, axr, ggs, ggr,
     xs_sem, xr_sem, ts_sem, tr_sem, ws_sem, wr_sem, zs_sem, zr_sem, gs_sem, gr_sem, hs_sem, hr_sem, cs_sem, cr_sem, go_sem,
 ):
     s = lax.axis_index("section")
@@ -48,14 +49,14 @@
     z, l = lax.div(t, 2), lax.rem(t, 2)
 
     def at_y(off, other=False):
-        return lax.rem(y + off, Y_RING) * 2 + (1 - h if other else h)
+        return lax.rem(y + off + Y_RING, Y_RING) * 2 + (1 - h if other else h)
 
     def at_z(off, other=False):
         return lax.rem(z + off + Z_RING, Z_RING) * 2 + (1 - l if other else l)
 
-    y_dev = [{"fsdp": at_y(o)} for o in OFFSETS]
+    y_dev = {way: {"fsdp": at_y(way)} for way in WAYS}
     x_dev = {"fsdp": at_y(0, True)}
-    up_dev, down_dev = {"tp": at_z(1)}, {"tp": at_z(-1)}
+    z_dev = {way: {"tp": at_z(way)} for way in WAYS}
     l_dev = {"tp": at_z(0, True)}
     core_dev = {"section": 1 - s}
 
@@ -65,10 +66,11 @@
     def f_rows(index, start=0, size=FS):
         return pl.ds(pl.multiple_of(index * FS + start, 16), size)
 
-    far_dev = [{"fsdp": at_y(o, True)} for o in OFFSETS]
-    f_devs = y_dev + [x_dev] + far_dev
+    f_devs = [{"fsdp": lax.rem(f + i, 2 * Y_RING)} for i in range(1, 2 * Y_RING)]
+    z_devs = [z_dev[1], z_dev[-1], l_dev]
+    cross = [{"section": 1 - s, **device} for device in z_devs]
     barrier = pltpu.get_barrier_semaphore()
-    peers = f_devs + [up_dev, down_dev, l_dev, core_dev]
+    peers = f_devs + z_devs + cross + [core_dev]
     for peer in peers:
         pl.semaphore_signal(barrier, inc=1, device_id=peer, device_id_type=MESH)
 
@@ -76,9 +78,7 @@
 
     @pl.when(s == 1)
     def _():
-        block = dy_ref[...].T
-        dy_all[t_rows(t), :] = block
-        dy_loc[...] = block
+        dy_all[t_rows(t), :] = dy_ref[...].T
 
     mine_w = f_rows(f)
     w_all[mine_w, 0:MAIN] = gate_ref[:, 0:MAIN]
@@ -111,11 +111,11 @@
 
         def out(self, way, k, j, q):
             i = (0 if way > 0 else 8) + 2 * k + j
-            return self.piece(at_z(-way * k, j == 1), i, q, up_dev if way > 0 else down_dev)
+            return self.piece(at_z(-way * k, j == 1), i, q, z_dev[way])
 
         def into(self, way, k, j, q):
             i = (0 if way > 0 else 8) + 2 * k + j
-            return self.piece(at_z(-way * (k + 1), j == 1), i, q, up_dev if way > 0 else down_dev)
+            return self.piece(at_z(-way * (k + 1), j == 1), i, q, z_dev[way])
 
         def pair(self, q, incoming=False):
             return self.piece(at_z(0, incoming), 16, q, l_dev)
@@ -141,73 +141,87 @@
                             if k < 3 and self.sends(way, k + 1, j):
                                 self.out(way, k + 1, j, q).start()
 
-        def drain(self):
+        def drain(self, handed=False):
             for q in range(PIECES):
                 for k in range(4):
                     for j in (0, 1):
                         for way in (1, -1):
-                            if self.sends(way, k, j):
+                            if self.sends(way, k, j) and not (handed and k == 0 and j == 0):
                                 self.out(way, k, j, q).wait_send()
-                self.pair(q).wait_send()
+                if not handed:
+                    self.pair(q).wait_send()
 
     ring_x = Ring(x_all, xs_sem, xr_sem)
     ring_t = Ring(dy_all, ts_sem, tr_sem)
 
-    def w_copy(rows, i, device):
-        return copy(w_all.at[rows], w_all.at[rows], ws_sem, wr_sem, i, device)
-
-    def w_full(d):
-        return w_copy(f_rows(f), d, y_dev[d])
-
-    def w_full_in(d):
-        return w_copy(f_rows(at_y(4 - OFFSETS[d])), d, y_dev[d])
-
-    def w_a(d):
-        return w_copy(f_rows(at_y(0, True), 0, PA), 3 + d, y_dev[d])
-
-    def w_a_in(d):
-        return w_copy(f_rows(at_y(4 - OFFSETS[d], True), 0, PA), 3 + d, y_dev[d])
-
-    def w_x():
-        return w_copy(f_rows(f), 6, x_dev)
-
-    def w_x_in():
-        return w_copy(f_rows(at_y(0, True)), 6, x_dev)
-
-    def w_b(d):
-        return w_copy(f_rows(at_y(4 - OFFSETS[d]), PA, PB), 7 + d, x_dev)
-
-    def w_b_in(d):
-        return w_copy(f_rows(at_y(4 - OFFSETS[d], True), PA, PB), 7 + d, x_dev)
-
-    def w_begin():
-        w_x().start()
-        for d in range(3):
-            w_full(d).start()
-
-    def w_middle():
-        w_x_in().wait_recv()
-        for d in range(3):
-            w_a(d).start()
-        for d in (0, 1):
-            w_full_in(d).wait_recv()
-            w_b(d).start()
-
-    def w_late():
-        w_full_in(2).wait_recv()
-        w_b(2).start()
-
-    def w_end():
-        for d in range(3):
-            w_a_in(d).wait_recv()
-            w_b_in(d).wait_recv()
-
-    def w_drain():
-        w_x().wait_send()
-        for d in range(3):
-            w_full(d).wait_send()
-            w_a(d).wait_send()
-            w_b(d).wait_send()
+    class Weights:
+        def __init__(self, p):
+            self.first = 12 * p
+            self.lanes = pl.ds(*LANES[p])
+
+        def copy(self, block, rows, i, device):
+            at = w_all.at[f_rows(block, *rows), self.lanes]
+            return copy(at, at, ws_sem, wr_sem, self.first + i, device)
+
+        def full(self, way, back=0):
+            return self.copy(at_y(-back * way), (0, FS), 0 if way > 0 else 1, y_dev[way])
+
+        def half(self, way, back=1):
+            rows = (0, FS // 2) if way > 0 else (FS // 2, FS // 2)
+            return self.copy(at_y(-back * way), rows, 2 if way > 0 else 3, y_dev[way])
+
+        def far(self, way, back=0):
+            return self.copy(at_y(-back * way, True), (0, PA), 4 if way > 0 else 5, y_dev[way])
+
+        def far_half(self, way, back=1):
+            rows = (0, PA // 2) if way > 0 else (PA // 2, PA // 2)
+            return self.copy(at_y(-back * way, True), rows, 6 if way > 0 else 7, y_dev[way])
+
+        def over(self, incoming=False):
+            return self.copy(at_y(0, incoming), (0, FS), 8, x_dev)
+
+        def late(self, i, incoming=False):
+            return self.copy(at_y((-1, 1, 2)[i], incoming), (PA, PB), 9 + i, x_dev)
+
+        def begin(self):
+            self.over().start()
+            for way in WAYS:
+                self.full(way).start()
+
+        def near(self):
+            for i, way in enumerate(WAYS):
+                self.full(way, 1).wait_recv()
+                self.half(way).start()
+                self.late(i).start()
+            self.over(True).wait_recv()
+            for way in WAYS:
+                self.far(way).start()
+
+        def next(self):
+            self.half(-1, 2).wait_recv()
+            self.late(2).start()
+            for way in WAYS:
+                self.far(way, 1).wait_recv()
+                self.far_half(way).start()
+
+        def end(self):
+            self.half(1, 2).wait_recv()
+            for way in WAYS:
+                self.far_half(way, 2).wait_recv()
+            for i in range(3):
+                self.late(i, True).wait_recv()
+
+        def drain(self):
+            self.over().wait_send()
+            for way in WAYS:
+                self.full(way).wait_send()
+                self.half(way).wait_send()
+                self.far(way).wait_send()
+                self.far_half(way).wait_send()
+            for i in range(3):
+                self.late(i).wait_send()
+
+    halves = [Weights(p) for p in range(len(LANES))]
 
     def columns():
         @pl.loop(0, DM // 128)
@@ -215,42 +229,49 @@
             lanes = pl.ds(pl.multiple_of(i * 128, 128), 128)
             gain_col[lanes, :] = jnp.broadcast_to(gain_ref[:, lanes], (128, 128)).T
 
-    @pl.when(s == 0)
-    def _():
-        columns()
+    def go(i):
+        pl.semaphore_signal(go_sem.at[i], inc=1, device_id=core_dev, device_id_type=MESH)
 
     @pl.when(s == 1)
     def _():
         ring_x.begin()
         ring_t.begin()
-        w_begin()
+        for one in halves:
+            one.begin()
         columns()
         ring_x.paired()
         ring_t.paired()
         ring_x.step(0)
+        halves[0].near()
         ring_t.step(0)
-        w_middle()
         ring_x.step(1)
+        halves[1].near()
+        go(0)
         ring_t.step(1)
         ring_x.step(2)
-        w_late()
+        halves[0].next()
         ring_t.step(2)
         ring_x.step(3)
+        halves[1].next()
         ring_t.step(3)
-        pl.semaphore_signal(go_sem.at[0], inc=1, device_id=core_dev, device_id_type=MESH)
 
     @pl.when(s == 0)
     def _():
+        columns()
         pl.semaphore_wait(go_sem.at[0], 1)
         ring_x.begin()
         ring_x.paired()
         ring_x.step(0)
+        ring_x.step(1)
         pl.semaphore_wait(go_sem.at[1], 1)
-        w_begin()
-        for k in (1, 2, 3):
-            ring_x.step(k)
-        w_middle()
-        w_late()
+        for one in halves:
+            one.begin()
+        ring_x.step(2)
+        ring_x.step(3)
+        for one in halves:
+            one.near()
+        for one in halves:
+            one.next()
 
     def wide(narrow):
         return jnp.concatenate([narrow] * (TOK // 128), axis=1)
@@ -268,11 +289,12 @@
         unit = x_all[rows, :].astype(F32) * scale[...]
         n_all[rows, :] = (unit * wide(gain_col[rows, :])).astype(BF16)
 
-    w_end()
+    for one in halves:
+        one.end()
 
     @pl.when(s == 1)
     def _():
-        pl.semaphore_signal(go_sem.at[1], inc=1, device_id=core_dev, device_id_type=MESH)
+        go(1)
 
     @pl.loop(0, PW // 128)
     def _(i):
@@ -300,14 +322,23 @@
     hid[MAIN + TAIL :, :] = jnp.zeros((DN - MAIN - TAIL, TOK), BF16)
     act[GU - 32 :, :] = jnp.zeros((32, TOK), BF16)
 
-    handed = copy(dx_t, dy_loc, cs_sem, cr_sem, 0, core_dev)
+    def handed(q):
+        rows = t_rows(t, q * PR, PR)
+        part = dx_t.at[pl.ds(q * PR, PR)]
+        made = [copy(part, dy_all.at[rows], cs_sem, cr_sem, q, core_dev)]
+        for n, i in enumerate((16, 0, 8)):
+            made.append(pltpu.make_async_remote_copy(
+                src_ref=part, dst_ref=dy_all.at[rows],
+                send_sem=cs_sem.at[(n + 1) * PIECES + q], recv_sem=tr_sem.at[i * PIECES + q],
+                device_id=(cross[2], cross[0], cross[1])[n], device_id_type=MESH,
+            ))
+        return made
 
     @pl.when(s == 0)
     def _():
-        handed.wait_recv()
-        dy_all[t_rows(t), :] = dy_loc[...]
-        ring_t.begin()
         ring_t.paired()
+        for q in range(PIECES):
+            handed(q)[0].wait_recv()
         for k in range(4):
             ring_t.step(k)
 
@@ -355,7 +386,7 @@
     def z_copy(way, k, j, q):
         i, rows = z_at(way, k, j), z_rows(j, q)
         part = pl.ds(rows.start, rows.stop - rows.start)
-        return copy(zs.at[i, part], zr.at[i, part], zs_sem, zr_sem, i * PIECES + q, up_dev if way > 0 else down_dev)
+        return copy(zs.at[i, part], zr.at[i, part], zs_sem, zr_sem, i * PIECES + q, z_dev[way])
 
     def z_step(k):
         for j, way in ((1, 1), (0, -1), (0, 1), (1, -1)):
@@ -378,7 +409,9 @@
                     zs[i, LW:, :] = stat_rows(total)
                 z_copy(way, k, j, q).start()
 
-    to_pair = copy(xls, xlr, zs_sem, zr_sem, 16 * PIECES, l_dev)
+    pair_rows, pair_stat = pl.ds(0, LW), pl.ds(LW, STAT)
+    to_pair = copy(xls.at[pair_rows], xlr.at[pair_rows], zs_sem, zr_sem, 16 * PIECES, l_dev)
+    to_pair_stat = copy(xls.at[pair_stat], xlr.at[pair_stat], zs_sem, zr_sem, 16 * PIECES + 1, l_dev)
 
     def z_end():
         for j in (1, 0):
@@ -393,18 +426,20 @@
                     total = total + stat_of(zr[i, LW:, :])
             if j == 1:
                 xls[:LW, :] = value.astype(BF16)
+                to_pair.start()
         xls[LW:, :] = stat_rows(total)
-        to_pair.start()
+        to_pair_stat.start()
         return value, total
 
     def finish(value, total):
         to_pair.wait_recv()
+        to_pair_stat.wait_recv()
         d_norm = value + xlr[:LW, :].astype(F32)
         norm_stat = (total + stat_of(xlr[LW:, :])) / DM
         mine = t_rows(t)
         unit = x_all[mine, :].astype(F32) * scale[...]
         dx_t[...] = (
-            dy_loc[...].astype(F32)
+            dy_all[mine, :].astype(F32)
             + scale[...] * (d_norm * wide(gain_col[mine, :]) - unit * norm_stat)
         ).astype(BF16)
         return d_norm * unit
@@ -420,106 +455,191 @@
         for one in gains:
             one.start()
 
-    def grads(rows):
-        return dot_t(n_all[rows, :], act[...]), dot_t(dy_all[rows, :], hid[...])
-
-    def g_x(o):
-        return copy(gsx.at[o], grx.at[o], gs_sem, gr_sem, o, x_dev)
-
-    def g_y(d):
-        return copy(gsy.at[d], gry.at[d], gs_sem, gr_sem, 4 + d, y_dev[d])
-
-    def g_y2(d):
-        return copy(g2y.at[d], r2y.at[d], gs_sem, gr_sem, 7 + d, y_dev[d])
-
-    def g_x2():
-        return copy(g2x, r2x, gs_sem, gr_sem, 10, x_dev)
-
-    def put(ref, lead, value):
-        ref[(*lead, slice(None), slice(0, GU))] = value[0].astype(ref.dtype)
-        ref[(*lead, slice(None), slice(GU, PW))] = value[1].astype(ref.dtype)
-
-    def grads_x(o):
-        put(gsx, (o,), grads(f_rows(at_y(o, True), PA, PB)))
-        g_x(o).start()
-
-    def grads_y(d):
-        put(gsy, (d, 0), grads(f_rows(at_y(OFFSETS[d]), 0, PA)))
-        put(gsy, (d, 1), grads(f_rows(at_y(OFFSETS[d], True), 0, PA)))
-        g_y(d).start()
-
-    def grads_all():
-        for o in (1, 3, 2, 0):
-            grads_x(o)
-        for d in range(3):
-            grads_y(d)
-
-        @pl.loop(0, Y_RING)
-        def _(o):
-            put(own_b, (o,), grads(f_rows(at_y(o), PA, PB)))
-
-        put(own_a, (0,), grads(f_rows(f, 0, PA)))
-        put(own_a, (1,), grads(f_rows(at_y(0, True), 0, PA)))
-
-    def second_b(d):
-        o = OFFSETS[d]
-        g_x(o).wait_recv()
-        g2y[d] = (own_b[o] + grx[o].astype(F32)).astype(BF16)
-        g_y2(d).start()
-
-    def second_a():
-        for d in range(3):
-            g_y(d).wait_recv()
-        g2x[...] = (
-            own_a[1] + gry[0, 1].astype(F32) + gry[1, 1].astype(F32) + gry[2, 1].astype(F32)
-        ).astype(BF16)
-        g_x2().start()
+    A_ROWS, B_ROWS = (0, PA), (PA, PB)
+    AH, BH = PA // 2, PB // 2
+    h_rows = {1: lambda n: pl.ds(0, n), -1: lambda n: pl.ds(n, n)}
+
+    class Grads:
+        def __init__(self, p):
+            self.p, self.first = p, 13 * p
+            self.start, self.width = LANES[p]
+            self.lanes = pl.ds(self.start, self.width)
+
+        def part(self, block, rows):
+            at = f_rows(block, *rows)
+            if self.p == 0:
+                return dot_t(n_all[at, :], act[: 2 * MAIN, :])
+            return jnp.concatenate(
+                [dot_t(n_all[at, :], act[2 * MAIN :, :]), dot_t(dy_all[at, :], hid[...])], axis=1
+            )
+
+        def copy(self, src, dst, index, i, device):
+            index = (*index, self.lanes)
+            return copy(src.at[index], dst.at[index], gs_sem, gr_sem, self.first + i, device)
+
+        def all(self, n):
+            return pl.ds(0, n)
+
+        def a_half(self, way):
+            return self.copy(ahs, ahr, (self.all(2), h_rows[way](AH)), 0 if way > 0 else 1, y_dev[way])
+
+        def a_full(self, way):
+            i = 0 if way > 0 else 1
+            return self.copy(afs, afr, (i, self.all(2), self.all(PA)), 2 + i, y_dev[way])
+
+        def b_over(self, o):
+            return self.copy(bxs, bxr, (o, self.all(PB)), 4 + o, x_dev)
+
+        def b_half(self, way):
+            return self.copy(bhs, bhr, (h_rows[way](BH),), 8 if way > 0 else 9, y_dev[way])
+
+        def b_full(self, way):
+            i = 0 if way > 0 else 1
+            return self.copy(bfs, bfr, (i, self.all(PB)), 10 + i, y_dev[way])
+
+        def a_over(self):
+            return self.copy(axs, axr, (self.all(PA),), 12, x_dev)
+
+        def begin(self):
+            for n in (0, 1):
+                ahs[n, :, self.lanes] = self.part(at_y(2, n == 1), A_ROWS).astype(BF16)
+            for way in WAYS:
+                self.a_half(way).start()
+            self.send_over(2)
+
+        def send_over(self, o):
+            bxs[o, :, self.lanes] = self.part(at_y(o, True), B_ROWS).astype(BF16)
+            self.b_over(o).start()
+
+        def rest(self):
+            for o in (1, 3, 0):
+                self.send_over(o)
+
+        def a_next(self):
+            for i, way in enumerate(WAYS):
+                self.a_half(way).wait_recv()
+                rows = h_rows[way](AH)
+                other = h_rows[-way](AH)
+                for n in (0, 1):
+                    value = self.part(at_y(way, n == 1), A_ROWS)
+                    mine = value[:AH] if way > 0 else value[AH:]
+                    rest = value[AH:] if way > 0 else value[:AH]
+                    afs[i, n, rows, self.lanes] = (mine + ahr[n, rows, self.lanes].astype(F32)).astype(BF16)
+                    afs[i, n, other, self.lanes] = rest.astype(BF16)
+                self.a_full(way).start()
+
+        def crossed(self, o):
+            self.b_over(o).wait_recv()
+            return self.part(at_y(o), B_ROWS) + bxr[o, :, self.lanes].astype(F32)
+
+        def b_next(self):
+            bhs[:, self.lanes] = self.crossed(2).astype(BF16)
+            for way in WAYS:
+                self.b_half(way).start()
+
+        def b_last(self):
+            for i, way in enumerate(WAYS):
+                value = self.crossed(1 if way > 0 else 3)
+                self.b_half(way).wait_recv()
+                rows = h_rows[way](BH)
+                other = h_rows[-way](BH)
+                mine = value[:BH] if way > 0 else value[BH:]
+                rest = value[BH:] if way > 0 else value[:BH]
+                bfs[i, rows, self.lanes] = (mine + bhr[rows, self.lanes].astype(F32)).astype(BF16)
+                bfs[i, other, self.lanes] = rest.astype(BF16)
+                self.b_full(way).start()
+
+        def a_sum(self, n):
+            return (
+                self.part(at_y(0, n == 1), A_ROWS)
+                + afr[0, n, :, self.lanes].astype(F32) + afr[1, n, :, self.lanes].astype(F32)
+            )
+
+        def a_last(self):
+            for way in WAYS:
+                self.a_full(way).wait_recv()
+            axs[:, self.lanes] = self.a_sum(1).astype(BF16)
+            self.a_over().start()
+
+        def result_a(self):
+            value = self.a_sum(0)
+            self.a_over().wait_recv()
+            return value + axr[:, self.lanes].astype(F32)
+
+        def result_b(self):
+            value = self.crossed(0)
+            for i, way in enumerate(WAYS):
+                self.b_full(way).wait_recv()
+                value = value + bfr[i, :, self.lanes].astype(F32)
+            return value
+
+        def drain(self):
+            for way in WAYS:
+                self.a_half(way).wait_send()
+                self.a_full(way).wait_send()
+                self.b_half(way).wait_send()
+                self.b_full(way).wait_send()
+            for o in range(4):
+                self.b_over(o).wait_send()
+            self.a_over().wait_send()
+
+    grads = [Grads(p) for p in range(len(LANES))]
+
+    def grads_begin():
+        for one in grads:
+            one.begin()
+        for one in grads:
+            one.rest()
 
     @pl.when(s == 1)
     def _():
         for k in range(4):
             z_step(k)
         terms = finish(*z_end())
-        handed.start()
+        for q in range(PIECES):
+            for one in handed(q):
+                one.start()
         send_gain(terms)
-        grads_all()
-        second_b(0)
-        second_b(1)
-        second_a()
-        second_b(2)
+        grads_begin()
+        for one in grads:
+            one.a_next()
+            one.b_next()
+        for one in grads:
+            one.a_last()
+            one.b_last()
 
     @pl.when(s == 0)
     def _():
-        grads_all()
+        grads_begin()
         z_step(0)
+        grads[0].a_next()
+        grads[0].b_next()
         z_step(1)
-        second_b(0)
+        grads[1].a_next()
+        grads[1].b_next()
         z_step(2)
-        second_b(1)
+        grads[0].a_last()
         z_step(3)
-        second_a()
-        second_b(2)
-        send_gain(finish(*z_end()))
+        grads[0].b_last()
+        ended = z_end()
+        grads[1].a_last()
+        grads[1].b_last()
+        send_gain(finish(*ended))
 
     dx_ref[...] = dx_t[...].T
 
-    def unpack(rows, value):
-        gate_grad[rows, :MAIN] = value[:, :MAIN]
-        up_grad[rows, :MAIN] = value[:, MAIN : 2 * MAIN]
-        gate_grad[rows, MAIN:] = value[:, 2 * MAIN : 2 * MAIN + TAIL]
-        up_grad[rows, MAIN:] = value[:, 2 * MAIN + TAIL : 2 * MAIN + 2 * TAIL]
-        down_grad[rows, :] = value[:, GU : GU + MAIN + TAIL]
-
-    g_x2().wait_recv()
-    unpack(slice(0, PA), (
-        own_a[0] + gry[0, 0].astype(F32) + gry[1, 0].astype(F32) + gry[2, 0].astype(F32) + r2x[...].astype(F32)
-    ))
-    g_x(0).wait_recv()
-    for d in range(3):
-        g_y2(d).wait_recv()
-    unpack(slice(PA, FS), (
-        own_b[0] + grx[0].astype(F32) + r2y[0].astype(F32) + r2y[1].astype(F32) + r2y[2].astype(F32)
-    ))
+    def unpack(rows, p, value):
+        if p == 0:
+            gate_grad[rows, :MAIN] = value[:, :MAIN]
+            up_grad[rows, :MAIN] = value[:, MAIN:]
+        else:
+            gate_grad[rows, MAIN:] = value[:, :TAIL]
+            up_grad[rows, MAIN:] = value[:, TAIL : 2 * TAIL]
+            down_grad[rows, :] = value[:, 128 : 128 + MAIN + TAIL]
+
+    for p, one in enumerate(grads):
+        unpack(slice(0, PA), p, one.result_a())
+        unpack(slice(PA, FS), p, one.result_b())
     summed = ggs[...]
     for i in range(7):
         gains[i].wait_recv()
@@ -527,8 +647,8 @@
     gain_grad[...] = summed[:1, :]
 
     ring_x.drain()
-    ring_t.drain()
-    w_drain()
+    for one in halves:
+        one.drain()
     for k in range(4):
         for j in (0, 1):
             for way in (1, -1):
@@ -536,18 +656,22 @@
                     for q in range(PIECES):
                         z_copy(way, k, j, q).wait_send()
     to_pair.wait_send()
-    for o in range(4):
-        g_x(o).wait_send()
-    for d in range(3):
-        g_y(d).wait_send()
-        g_y2(d).wait_send()
-    g_x2().wait_send()
+    to_pair_stat.wait_send()
+    for one in grads:
+        one.drain()
     for one in gains:
         one.wait_send()
 
     @pl.when(s == 1)
     def _():
-        handed.wait_send()
+        ring_t.drain()
+        for q in range(PIECES):
+            for one in handed(q):
+                one.wait_send()
+
+    @pl.when(s == 0)
+    def _():
+        ring_t.drain(True)
 
 
 def window(*args):
@@ -573,7 +697,6 @@
             pltpu.VMEM((DM, PW), BF16),
             pltpu.VMEM((PW, DM), BF16),
             pltpu.VMEM((LW, TOK), BF16),
-            pltpu.VMEM((LW, TOK), BF16),
             pltpu.VMEM((DM, 128), F32),
             pltpu.VMEM((GU, TOK), F32),
             pltpu.VMEM((GU, TOK), F32),
@@ -585,20 +708,22 @@
             pltpu.VMEM((16, LW + STAT, TOK), BF16),
             pltpu.VMEM((LW + STAT, TOK), BF16),
             pltpu.VMEM((LW + STAT, TOK), BF16),
+            pltpu.VMEM((2, PA, PW), BF16),
+            pltpu.VMEM((2, PA, PW), BF16),
+            pltpu.VMEM((2, 2, PA, PW), BF16),
+            pltpu.VMEM((2, 2, PA, PW), BF16),
             pltpu.VMEM((4, PB, PW), BF16),
             pltpu.VMEM((4, PB, PW), BF16),
-            pltpu.VMEM((3, 2, PA, PW), BF16),
-            pltpu.VMEM((3, 2, PA, PW), BF16),
-            pltpu.VMEM((3, PB, PW), BF16),
-            pltpu.VMEM((3, PB, PW), BF16),
+            pltpu.VMEM((PB, PW), BF16),
+            pltpu.VMEM((PB, PW), BF16),
+            pltpu.VMEM((2, PB, PW), BF16),
+            pltpu.VMEM((2, PB, PW), BF16),
             pltpu.VMEM((PA, PW), BF16),
             pltpu.VMEM((PA, PW), BF16),
-            pltpu.VMEM((4, PB, PW), F32),
-            pltpu.VMEM((2, PA, PW), F32),
             pltpu.VMEM((8, LW), F32),
             pltpu.VMEM((7, 8, LW), F32),
-            ring, ring, ring, ring, dma((10,)), dma((10,)),
-            ring, ring, dma((11,)), dma((11,)), dma((7,)), dma((7,)), dma((1,)), dma((1,)),
+            ring, ring, ring, ring, dma((24,)), dma((24,)),
+            ring, ring, dma((26,)), dma((26,)), dma((7,)), dma((7,)), dma((4 * PIECES,)), dma((PIECES,)),
             pltpu.SemaphoreType.REGULAR((2,)),
         ],
         compiler_params=pltpu.CompilerParams(

time: 175 us -> 145 us (0.83)
  Pallas kernels: 167 us -> 138 us
    pallas_call x1, Pallas kernels: 167 us -> 138 us  [window(): pl.pallas_call(kernel, name='window', out_shape=(jax.ShapeDtypeStruct((TO...]
where the time goes in v2:
time: 145 us
  Pallas kernels  138 us (95%)
  local copies, waits for them, and re-layouts  6.43 us (4%)
    pallas_call x1, Pallas kernels, window(): pl.pallas_call(kernel, name='window', out_shape=(jax.ShapeDtypeStruct((TO...  138 us
    unnamed x11, local copies, waits for them, and re-layouts  6.43 us

profile of v2, /device:TPU:8, one launch (start us, length us, event | category | flops | bytes accessed | tf_op | source)
XLA Modules:
  0.0 144.9 jit_solution(11438677450312950506)
XLA Ops:
  0.6 137.8 %window.1 = (bf16[512,160]{1,0:T(8,128)(2,1)}, f32[320,432]{1,0:T(8,128)}, f32[320,432]{1,0:T(8,128)}, f32[320,432]{1,0:T(8,128)}, f32[1,160]{1,0:T(1,128)}) custom-call(bf16[512,160]{1,0:T(8,128)(2,1)} %bitcast.20, bf16[512,160]{1,0:T(8,128)(2,1)} %bitcast.21, f32[1,2560]{1,0:T(1,128)} %gain_ref.1, bf16[320,432]{1,0:T(8,128)(2,1)} %bitcast.16, ...), custom_call_target="tpu_custom_call" | custom-call | tf_op jit(solution)/shard_map/window/pallas_call | solution.py:681
  138.5 1.7 %copy.16 = bf16[1,8,64,160]{3,2,1,0:T(8,128)(2,1)} copy(bf16[1,8,64,160]{3,2,1,0:T(8,128)(2,1)} %bitcast.19) | data formatting | bytes 327680
  140.1 0.0 copy-start.1
  140.1 2.0 %copy.17 = f32[1,320,432]{2,1,0:T(8,128)} copy(f32[1,320,432]{2,1,0:T(8,128)} %bitcast.15) | data formatting | bytes 1105920
  142.2 0.0 copy-done.1
  142.2 0.0 copy-start
  142.2 0.8 copy.18
  143.0 0.5 copy-done
  143.5 0.0 copy-start.2
  143.5 0.8 copy.19
  144.3 0.0 copy-done.2
  144.3 0.6 copy.20
Async XLA Ops:
  140.1 2.0 %copy-start.1 = (f32[320,432]{1,0:T(8,128)S(1)}, f32[320,432]{1,0:T(8,128)}, u32[]{:S(2)}) copy-start(f32[320,432]{1,0:T(8,128)} %get-tuple-element.12) | copy-start | bytes 1658884
  142.2 1.3 copy-start
  143.5 0.8 copy-start.2

commit v3 on v2

--- a/solution.py
+++ b/solution.py
@@ -36,9 +36,11 @@
 
 
 def kernel(
-    x_ref, dy_ref, gain_ref, gate_ref, up_ref, down_ref,
-    dx_ref, gate_grad, up_grad, down_grad, gain_grad,
-    x_all, dy_all, n_all, w_all, w_t, dx_t, gain_col, gu, fac, hid, act, scale, stat,
+    x_in, dy_in, gain_in, gate_in, up_in, down_in,
+    dx_out, gate_out, up_out, down_out, gain_out,
+    x_ref, dy_ref, gain_ref, gate_ref, up_ref, down_ref, in_sem,
+    dx_ref, gate_grad, up_grad, down_grad, gain_grad, out_sem,
+    x_all, dy_all, n_all, w_all, w_t, dx_t, gain_col, gu, fac, hid, act, d_hid, scale, stat,
     zs, zr, xls, xlr, ahs, ahr, afs, afr, bxs, bxr, bhs, bhr, bfs, bfr, axs, axr, ggs, ggr,
     xs_sem, xr_sem, ts_sem, tr_sem, ws_sem, wr_sem, zs_sem, zr_sem, gs_sem, gr_sem, hs_sem, hr_sem, cs_sem, cr_sem, go_sem,
 ):
@@ -73,6 +75,17 @@
     peers = f_devs + z_devs + cross + [core_dev]
     for peer in peers:
         pl.semaphore_signal(barrier, inc=1, device_id=peer, device_id_type=MESH)
+
+    reads = [
+        pltpu.make_async_copy(src, dst, in_sem.at[i])
+        for i, (src, dst) in enumerate((
+            (x_in, x_ref), (gate_in, gate_ref), (up_in, up_ref), (down_in, down_ref), (gain_in, gain_ref), (dy_in, dy_ref),
+        ))
+    ]
+    for read in reads:
+        read.start()
+    for read in reads:
+        read.wait()
 
     x_all[t_rows(t), :] = x_ref[...].T
 
@@ -94,7 +107,7 @@
 
     def copy(src, dst, send, recv, i, device):
         return pltpu.make_async_remote_copy(
-            src_ref=src, dst_ref=dst, send_sem=send.at[i], recv_sem=recv.at[i],
+            src_ref=src, dst_ref=dst, send_sem=send, recv_sem=recv.at[i],
             device_id=device, device_id_type=MESH,
         )
 
@@ -123,6 +136,9 @@
         def begin(self):
             for q in range(PIECES):
                 self.pair(q).start()
+
+        def begin_z(self):
+            for q in range(PIECES):
                 self.out(1, 0, 0, q).start()
                 self.out(-1, 0, 0, q).start()
 
@@ -141,15 +157,9 @@
                             if k < 3 and self.sends(way, k + 1, j):
                                 self.out(way, k + 1, j, q).start()
 
-        def drain(self, handed=False):
-            for q in range(PIECES):
-                for k in range(4):
-                    for j in (0, 1):
-                        for way in (1, -1):
-                            if self.sends(way, k, j) and not (handed and k == 0 and j == 0):
-                                self.out(way, k, j, q).wait_send()
-                if not handed:
-                    self.pair(q).wait_send()
+        def drain(self, blocks):
+            block = self.whole.at[pl.ds(0, blocks * LW)]
+            copy(block, block, self.send, self.recv, 0, l_dev).wait_send()
 
     ring_x = Ring(x_all, xs_sem, xr_sem)
     ring_t = Ring(dy_all, ts_sem, tr_sem)
@@ -157,11 +167,12 @@
     class Weights:
         def __init__(self, p):
             self.first = 12 * p
+            self.send = ws_sem.at[p]
             self.lanes = pl.ds(*LANES[p])
 
         def copy(self, block, rows, i, device):
             at = w_all.at[f_rows(block, *rows), self.lanes]
-            return copy(at, at, ws_sem, wr_sem, self.first + i, device)
+            return copy(at, at, self.send, wr_sem, self.first + i, device)
 
         def full(self, way, back=0):
             return self.copy(at_y(-back * way), (0, FS), 0 if way > 0 else 1, y_dev[way])
@@ -204,22 +215,19 @@
                 self.far(way, 1).wait_recv()
                 self.far_half(way).start()
 
+        def side(self, way):
+            self.late(0 if way > 0 else 1, True).wait_recv()
+
         def end(self):
             self.half(1, 2).wait_recv()
             for way in WAYS:
                 self.far_half(way, 2).wait_recv()
-            for i in range(3):
-                self.late(i, True).wait_recv()
+            self.late(2, True).wait_recv()
 
         def drain(self):
-            self.over().wait_send()
-            for way in WAYS:
-                self.full(way).wait_send()
-                self.half(way).wait_send()
-                self.far(way).wait_send()
-                self.far_half(way).wait_send()
-            for i in range(3):
-                self.late(i).wait_send()
+            rows = 3 * FS + FS + 3 * PA + 3 * PB
+            block = w_all.at[pl.ds(0, rows), self.lanes]
+            copy(block, block, self.send, wr_sem, 0, x_dev).wait_send()
 
     halves = [Weights(p) for p in range(len(LANES))]
 
@@ -235,31 +243,31 @@
     @pl.when(s == 1)
     def _():
         ring_x.begin()
+        ring_x.begin_z()
+        halves[0].begin()
         ring_t.begin()
-        for one in halves:
-            one.begin()
+        halves[1].begin()
         columns()
         ring_x.paired()
+        ring_x.step(0)
+        ring_t.begin_z()
         ring_t.paired()
-        ring_x.step(0)
         halves[0].near()
-        ring_t.step(0)
         ring_x.step(1)
         halves[1].near()
-        go(0)
-        ring_t.step(1)
+        ring_t.step(0)
         ring_x.step(2)
         halves[0].next()
-        ring_t.step(2)
+        ring_t.step(1)
+        go(0)
         ring_x.step(3)
-        halves[1].next()
-        ring_t.step(3)
 
     @pl.when(s == 0)
     def _():
+        ring_x.begin()
         columns()
         pl.semaphore_wait(go_sem.at[0], 1)
-        ring_x.begin()
+        ring_x.begin_z()
         ring_x.paired()
         ring_x.step(0)
         ring_x.step(1)
@@ -270,8 +278,7 @@
         ring_x.step(3)
         for one in halves:
             one.near()
-        for one in halves:
-            one.next()
+        halves[0].next()
 
     def wide(narrow):
         return jnp.concatenate([narrow] * (TOK // 128), axis=1)
@@ -289,6 +296,33 @@
         unit = x_all[rows, :].astype(F32) * scale[...]
         n_all[rows, :] = (unit * wide(gain_col[rows, :])).astype(BF16)
 
+    def gate_up(block, first):
+        cols = pl.ds(pl.multiple_of(lax.rem(block, Y_RING) * 2 * FS, 128), 2 * FS)
+        for i in range(PW // 128):
+            lanes = slice(i * 128, (i + 1) * 128)
+            w_t[lanes, cols] = w_all[cols, lanes].T
+
+        @pl.loop(0, 2)
+        def _(i):
+            rows = pl.ds(pl.multiple_of(i * (GU // 2), 64), GU // 2)
+            value = dot(w_t[rows, cols], n_all[cols, :])
+            gu[rows, :] = value if first else gu[rows, :] + value
+
+    halves[1].next()
+    gate_up(y, True)
+
+    @pl.when(s == 1)
+    def _():
+        ring_t.step(2)
+
+    for way in WAYS:
+        for one in halves:
+            one.side(way)
+
+    @pl.loop(0, 2)
+    def _(i):
+        gate_up(y + 1 + 2 * i, False)
+
     for one in halves:
         one.end()
 
@@ -296,16 +330,7 @@
     def _():
         go(1)
 
-    @pl.loop(0, PW // 128)
-    def _(i):
-        lanes = pl.ds(pl.multiple_of(i * 128, 128), 128)
-        for k in range(Y_RING):
-            w_t[lanes, 640 * k : 640 * (k + 1)] = w_all[640 * k : 640 * (k + 1), lanes].T
-
-    @pl.loop(0, 2)
-    def _(i):
-        rows = pl.ds(pl.multiple_of(i * (GU // 2), 64), GU // 2)
-        gu[rows, :] = dot(w_t[rows, :], n_all[...])
+    gate_up(y + 2, False)
 
     spans = ((0, MAIN, MAIN, 0), (2 * MAIN, 2 * MAIN + TAIL, TAIL, MAIN))
 
@@ -325,7 +350,7 @@
     def handed(q):
         rows = t_rows(t, q * PR, PR)
         part = dx_t.at[pl.ds(q * PR, PR)]
-        made = [copy(part, dy_all.at[rows], cs_sem, cr_sem, q, core_dev)]
+        made = [copy(part, dy_all.at[rows], cs_sem.at[q], cr_sem, q, core_dev)]
         for n, i in enumerate((16, 0, 8)):
             made.append(pltpu.make_async_remote_copy(
                 src_ref=part, dst_ref=dy_all.at[rows],
@@ -339,10 +364,21 @@
         ring_t.paired()
         for q in range(PIECES):
             handed(q)[0].wait_recv()
-        for k in range(4):
+        for k in range(3):
             ring_t.step(k)
 
-    d_hid = dot(w_t[GU:, :], dy_all[...])
+    def hidden_back(block):
+        cols = pl.ds(pl.multiple_of(lax.rem(block, Z_RING // 2) * 4 * LW, 128), 4 * LW)
+        return dot(w_t[GU:, cols], dy_all[cols, :])
+
+    d_hid[...] = hidden_back(lax.div(z, 2))
+
+    @pl.loop(0, 2)
+    def _(i):
+        d_hid[...] += hidden_back(lax.div(z, 2) + 1 + 2 * i)
+
+    ring_t.step(3)
+    d_hid[...] += hidden_back(lax.div(z, 2) + 2)
 
     def back(gate_at, up_at, size, at):
         grad = d_hid[at : at + size, :]
@@ -389,7 +425,7 @@
         return copy(zs.at[i, part], zr.at[i, part], zs_sem, zr_sem, i * PIECES + q, z_dev[way])
 
     def z_step(k):
-        for j, way in ((1, 1), (0, -1), (0, 1), (1, -1)):
+        for j, way in ((1, 1), (0, -1), (1, -1), (0, 1)) if k < 2 else ((1, 1), (1, -1), (0, 1), (0, -1)):
             if not z_has(way, k, j):
                 continue
             value = partial(way * (4 - k), j)
@@ -409,31 +445,35 @@
                     zs[i, LW:, :] = stat_rows(total)
                 z_copy(way, k, j, q).start()
 
-    pair_rows, pair_stat = pl.ds(0, LW), pl.ds(LW, STAT)
-    to_pair = copy(xls.at[pair_rows], xlr.at[pair_rows], zs_sem, zr_sem, 16 * PIECES, l_dev)
-    to_pair_stat = copy(xls.at[pair_stat], xlr.at[pair_stat], zs_sem, zr_sem, 16 * PIECES + 1, l_dev)
+    def to_pair(q):
+        rows = pl.ds(q * PR, PR) if q < PIECES else pl.ds(LW, STAT)
+        return copy(xls.at[rows], xlr.at[rows], zs_sem, zr_sem, 16 * PIECES + q, l_dev)
 
     def z_end():
-        for j in (1, 0):
-            value = partial(0, j)
-            total = stat[...]
-            for way in (1, -1):
-                i = z_at(way, 3, j)
-                for q in range(PIECES):
-                    z_copy(way, 3, j, q).wait_recv()
-                value = value + zr[i, :LW, :].astype(F32)
-                if j == 0:
-                    total = total + stat_of(zr[i, LW:, :])
-            if j == 1:
-                xls[:LW, :] = value.astype(BF16)
-                to_pair.start()
+        value = partial(0, 1)
+        for q in range(PIECES):
+            rows = slice(q * PR, (q + 1) * PR)
+            part = value[rows, :]
+            for way in WAYS:
+                z_copy(way, 3, 1, q).wait_recv()
+                part = part + zr[z_at(way, 3, 1), rows, :].astype(F32)
+            xls[rows, :] = part.astype(BF16)
+            to_pair(q).start()
+        value = partial(0, 0)
+        total = stat[...]
+        for way in WAYS:
+            i = z_at(way, 3, 0)
+            for q in range(PIECES):
+                z_copy(way, 3, 0, q).wait_recv()
+            value = value + zr[i, :LW, :].astype(F32)
+            total = total + stat_of(zr[i, LW:, :])
         xls[LW:, :] = stat_rows(total)
-        to_pair_stat.start()
+        to_pair(PIECES).start()
         return value, total
 
     def finish(value, total):
-        to_pair.wait_recv()
-        to_pair_stat.wait_recv()
+        for q in range(PIECES + 1):
+            to_pair(q).wait_recv()
         d_norm = value + xlr[:LW, :].astype(F32)
         norm_stat = (total + stat_of(xlr[LW:, :])) / DM
         mine = t_rows(t)
@@ -444,7 +484,7 @@
         ).astype(BF16)
         return d_norm * unit
 
-    gains = [copy(ggs, ggr.at[i], hs_sem, hr_sem, i, f_devs[i]) for i in range(7)]
+    gains = [copy(ggs, ggr.at[i], hs_sem.at[i], hr_sem, i, f_devs[i]) for i in range(7)]
 
     def send_gain(terms):
         lanes = terms[:, :128] + terms[:, 128:256] + terms[:, 256:384] + terms[:, 384:]
@@ -461,7 +501,7 @@
 
     class Grads:
         def __init__(self, p):
-            self.p, self.first = p, 13 * p
+            self.p, self.first, self.send = p, 13 * p, gs_sem.at[p]
             self.start, self.width = LANES[p]
             self.lanes = pl.ds(self.start, self.width)
 
@@ -475,7 +515,7 @@
 
         def copy(self, src, dst, index, i, device):
             index = (*index, self.lanes)
-            return copy(src.at[index], dst.at[index], gs_sem, gr_sem, self.first + i, device)
+            return copy(src.at[index], dst.at[index], self.send, gr_sem, self.first + i, device)
 
         def all(self, n):
             return pl.ds(0, n)
@@ -561,27 +601,19 @@
             axs[:, self.lanes] = self.a_sum(1).astype(BF16)
             self.a_over().start()
 
-        def result_a(self):
-            value = self.a_sum(0)
+        def arrived_a(self):
             self.a_over().wait_recv()
-            return value + axr[:, self.lanes].astype(F32)
-
-        def result_b(self):
-            value = self.crossed(0)
-            for i, way in enumerate(WAYS):
+            return axr[:, self.lanes].astype(F32)
+
+        def arrived_b(self):
+            for way in WAYS:
                 self.b_full(way).wait_recv()
-                value = value + bfr[i, :, self.lanes].astype(F32)
-            return value
+            return bfr[0, :, self.lanes].astype(F32) + bfr[1, :, self.lanes].astype(F32)
 
         def drain(self):
-            for way in WAYS:
-                self.a_half(way).wait_send()
-                self.a_full(way).wait_send()
-                self.b_half(way).wait_send()
-                self.b_full(way).wait_send()
-            for o in range(4):
-                self.b_over(o).wait_send()
-            self.a_over().wait_send()
+            rows = 2 * PA + 4 * PA + 4 * PB + PB + 2 * PB + PA
+            block = w_all.at[pl.ds(0, rows), self.lanes]
+            copy(block, block, self.send, gr_sem, 0, x_dev).wait_send()
 
     grads = [Grads(p) for p in range(len(LANES))]
 
@@ -590,6 +622,20 @@
             one.begin()
         for one in grads:
             one.rest()
+
+    def unpack(rows, p, value, add=False):
+        def put(ref, lanes, part):
+            ref[rows, lanes] = ref[rows, lanes] + part if add else part
+
+        if p == 0:
+            put(gate_grad, slice(0, MAIN), value[:, :MAIN])
+            put(up_grad, slice(0, MAIN), value[:, MAIN:])
+        else:
+            put(gate_grad, slice(MAIN, MAIN + TAIL), value[:, :TAIL])
+            put(up_grad, slice(MAIN, MAIN + TAIL), value[:, TAIL : 2 * TAIL])
+            put(down_grad, slice(0, MAIN + TAIL), value[:, 128 : 128 + MAIN + TAIL])
+
+    top, rest = slice(0, PA), slice(PA, FS)
 
     @pl.when(s == 1)
     def _():
@@ -600,63 +646,71 @@
             for one in handed(q):
                 one.start()
         send_gain(terms)
-        grads_begin()
         for one in grads:
+            one.begin()
+        for one in grads:
+            one.rest()
+        for one in grads:
+            one.b_next()
             one.a_next()
-            one.b_next()
+        for p, one in enumerate(grads):
+            one.b_last()
+            unpack(rest, p, one.crossed(0))
+        for p, one in enumerate(grads):
+            one.a_last()
+            unpack(top, p, one.a_sum(0))
+
+    @pl.when(s == 0)
+    def _():
+        grads[0].begin()
+        z_step(0)
+        grads[1].begin()
         for one in grads:
-            one.a_last()
-            one.b_last()
-
-    @pl.when(s == 0)
-    def _():
-        grads_begin()
-        z_step(0)
+            one.rest()
+        z_step(1)
+        grads[0].b_next()
         grads[0].a_next()
-        grads[0].b_next()
-        z_step(1)
+        z_step(2)
+        grads[1].b_next()
         grads[1].a_next()
-        grads[1].b_next()
-        z_step(2)
+        grads[0].b_last()
+        z_step(3)
         grads[0].a_last()
-        z_step(3)
-        grads[0].b_last()
+        unpack(top, 0, grads[0].a_sum(0))
+        grads[1].b_last()
         ended = z_end()
+        unpack(rest, 0, grads[0].crossed(0))
+        unpack(rest, 1, grads[1].crossed(0))
         grads[1].a_last()
-        grads[1].b_last()
         send_gain(finish(*ended))
+        unpack(top, 1, grads[1].a_sum(0))
 
     dx_ref[...] = dx_t[...].T
-
-    def unpack(rows, p, value):
-        if p == 0:
-            gate_grad[rows, :MAIN] = value[:, :MAIN]
-            up_grad[rows, :MAIN] = value[:, MAIN:]
-        else:
-            gate_grad[rows, MAIN:] = value[:, :TAIL]
-            up_grad[rows, MAIN:] = value[:, TAIL : 2 * TAIL]
-            down_grad[rows, :] = value[:, 128 : 128 + MAIN + TAIL]
+    writes = [
+        pltpu.make_async_copy(src, dst, out_sem.at[i])
+        for i, (src, dst) in enumerate((
+            (dx_ref, dx_out), (gate_grad, gate_out), (up_grad, up_out), (down_grad, down_out), (gain_grad, gain_out),
+        ))
+    ]
+    writes[0].start()
 
     for p, one in enumerate(grads):
-        unpack(slice(0, PA), p, one.result_a())
-        unpack(slice(PA, FS), p, one.result_b())
+        unpack(top, p, one.arrived_a(), True)
+        unpack(rest, p, one.arrived_b(), True)
     summed = ggs[...]
     for i in range(7):
         gains[i].wait_recv()
         summed = summed + ggr[i]
     gain_grad[...] = summed[:1, :]
-
-    ring_x.drain()
+    for one in writes[1:]:
+        one.start()
+
+    ring_x.drain(15)
     for one in halves:
         one.drain()
-    for k in range(4):
-        for j in (0, 1):
-            for way in (1, -1):
-                if z_has(way, k, j):
-                    for q in range(PIECES):
-                        z_copy(way, k, j, q).wait_send()
-    to_pair.wait_send()
-    to_pair_stat.wait_send()
+    z_rows_sent = 15 * LW + 8 * STAT
+    block = x_all.at[pl.ds(0, z_rows_sent)]
+    copy(block, block, zs_sem, zr_sem, 0, l_dev).wait_send()
     for one in grads:
         one.drain()
     for one in gains:
@@ -664,33 +718,56 @@
 
     @pl.when(s == 1)
     def _():
-        ring_t.drain()
+        ring_t.drain(15)
         for q in range(PIECES):
             for one in handed(q):
                 one.wait_send()
 
     @pl.when(s == 0)
     def _():
-        ring_t.drain(True)
+        ring_t.drain(12)
+
+    for one in writes:
+        one.wait()
+
+
+def write(*refs):
+    count = len(refs) // 3
+    reads, writes = [
+        [pltpu.make_async_copy(refs[a + i], refs[b + i], refs[-1].at[c + i]) for i in range(count)]
+        for a, b, c in ((0, 2 * count, 0), (2 * count, count, count))
+    ]
+    for one in reads:
+        one.start()
+    for one, other in zip(reads, writes):
+        one.wait()
+        other.start()
+    for one in writes:
+        one.wait()
 
 
 def window(*args):
-    vmem = pl.BlockSpec(memory_space=pltpu.VMEM)
+    hbm = pl.BlockSpec(memory_space=pltpu.HBM)
     dma = pltpu.SemaphoreType.DMA
-    ring = dma((17 * PIECES,))
-    return pl.pallas_call(
+    ring = dma((17 * PIECES + 1,))
+    shapes = (
+        jax.ShapeDtypeStruct((TOK, LW), BF16),
+        jax.ShapeDtypeStruct((FS, MAIN + TAIL), F32),
+        jax.ShapeDtypeStruct((FS, MAIN + TAIL), F32),
+        jax.ShapeDtypeStruct((FS, MAIN + TAIL), F32),
+        jax.ShapeDtypeStruct((1, LW), F32),
+    )
+    results = pl.pallas_call(
         kernel,
         name="window",
-        out_shape=(
-            jax.ShapeDtypeStruct((TOK, LW), BF16),
-            jax.ShapeDtypeStruct((FS, MAIN + TAIL), F32),
-            jax.ShapeDtypeStruct((FS, MAIN + TAIL), F32),
-            jax.ShapeDtypeStruct((FS, MAIN + TAIL), F32),
-            jax.ShapeDtypeStruct((1, LW), F32),
-        ),
-        in_specs=[vmem] * 6,
-        out_specs=(vmem,) * 5,
+        out_shape=shapes,
+        in_specs=[hbm] * 6,
+        out_specs=(hbm,) * 5,
         scratch_shapes=[
+            *(pltpu.VMEM(arg.shape, arg.dtype) for arg in args),
+            dma((6,)),
+            *(pltpu.VMEM(shape.shape, shape.dtype) for shape in shapes),
+            dma((5,)),
             pltpu.VMEM((DM, TOK), BF16),
             pltpu.VMEM((DM, TOK), BF16),
             pltpu.VMEM((DM, TOK), BF16),
@@ -702,34 +779,38 @@
             pltpu.VMEM((GU, TOK), F32),
             pltpu.VMEM((DN, TOK), BF16),
             pltpu.VMEM((GU, TOK), BF16),
+            pltpu.VMEM((DN, TOK), F32),
             pltpu.VMEM((1, TOK), F32),
             pltpu.VMEM((1, TOK), F32),
             pltpu.VMEM((16, LW + STAT, TOK), BF16),
             pltpu.VMEM((16, LW + STAT, TOK), BF16),
             pltpu.VMEM((LW + STAT, TOK), BF16),
             pltpu.VMEM((LW + STAT, TOK), BF16),
-            pltpu.VMEM((2, PA, PW), BF16),
-            pltpu.VMEM((2, PA, PW), BF16),
-            pltpu.VMEM((2, 2, PA, PW), BF16),
-            pltpu.VMEM((2, 2, PA, PW), BF16),
-            pltpu.VMEM((4, PB, PW), BF16),
-            pltpu.VMEM((4, PB, PW), BF16),
-            pltpu.VMEM((PB, PW), BF16),
-            pltpu.VMEM((PB, PW), BF16),
-            pltpu.VMEM((2, PB, PW), BF16),
-            pltpu.VMEM((2, PB, PW), BF16),
-            pltpu.VMEM((PA, PW), BF16),
-            pltpu.VMEM((PA, PW), BF16),
+            *(pltpu.VMEM((2, PA, PW), BF16),) * 2,
+            *(pltpu.VMEM((2, 2, PA, PW), BF16),) * 2,
+            *(pltpu.VMEM((4, PB, PW), BF16),) * 2,
+            *(pltpu.VMEM((PB, PW), BF16),) * 2,
+            *(pltpu.VMEM((2, PB, PW), BF16),) * 2,
+            *(pltpu.VMEM((PA, PW), BF16),) * 2,
             pltpu.VMEM((8, LW), F32),
             pltpu.VMEM((7, 8, LW), F32),
-            ring, ring, ring, ring, dma((24,)), dma((24,)),
-            ring, ring, dma((26,)), dma((26,)), dma((7,)), dma((7,)), dma((4 * PIECES,)), dma((PIECES,)),
+            dma, ring, dma, ring, dma((2,)), dma((24,)),
+            dma, ring, dma((2,)), dma((26,)), dma((7,)), dma((7,)), dma((4 * PIECES,)), dma((PIECES,)),
             pltpu.SemaphoreType.REGULAR((2,)),
         ],
         compiler_params=pltpu.CompilerParams(
-            collective_id=0, has_side_effects=True, vmem_limit_bytes=67043328
+            collective_id=0, has_side_effects=True, vmem_limit_bytes=58 * 1024 * 1024
         ),
     )(*args)
+    return pl.pallas_call(
+        write,
+        name="write",
+        out_shape=shapes,
+        in_specs=[hbm] * 5,
+        out_specs=(hbm,) * 5,
+        scratch_shapes=[*(pltpu.VMEM(shape.shape, shape.dtype) for shape in shapes), dma((10,))],
+        compiler_params=pltpu.CompilerParams(vmem_limit_bytes=67043328),
+    )(*results)
 
 
 def shards(saved_inputs, top_grad, norm_gain, gate_weight, up_weight, down_weight):

time: 145 us -> 133 us (0.917)
  Pallas kernels: 138 us -> 131 us
  local copies, waits for them, and re-layouts: 6.43 us -> 0 us
    unnamed x11 -> x0, local copies, waits for them, and re-layouts: 6.43 us -> none
    pallas_call x1 -> x2, Pallas kernels: 138 us -> 131 us  [the longest x1 129 us: window(): pl.pallas_call(kernel, name='window', out_shape=shapes, in_specs=[hbm] *...]
where the time goes in v3:
time: 133 us; the launch traced here: 132 us
  Pallas kernels  131 us (98%)
    pallas_call x1, Pallas kernels, window(): pl.pallas_call(kernel, name='window', out_shape=shapes, in_specs=[hbm] *...  129 us

profile of v3, /device:TPU:8, one launch (start us, length us, event | category | flops | bytes accessed | tf_op | source)
XLA Modules:
  0.0 132.3 jit_solution(7486689584884592517)
XLA Ops:
  0.6 129.0 %window.1 = (bf16[512,160]{1,0:T(8,128)(2,1)}, f32[320,432]{1,0:T(8,128)}, f32[320,432]{1,0:T(8,128)}, f32[320,432]{1,0:T(8,128)}, f32[1,160]{1,0:T(1,128)}) custom-call(bf16[512,160]{1,0:T(8,128)(2,1)} %bitcast.16, bf16[512,160]{1,0:T(8,128)(2,1)} %bitcast.17, f32[1,2560]{1,0:T(1,128)} %gain_in.1, bf16[320,432]{1,0:T(8,128)(2,1)} %bitcast.13, ...), custom_call_target="tpu_custom_call" | custom-call | tf_op jit(solution)/shard_map/window/pallas_call | solution.py:760
  129.6 2.5 %write.1 = (bf16[512,160]{1,0:T(8,128)(2,1)}, f32[320,432]{1,0:T(8,128)}, f32[320,432]{1,0:T(8,128)}, f32[320,432]{1,0:T(8,128)}, f32[1,160]{1,0:T(1,128)}) custom-call(bf16[512,160]{1,0:T(8,128)(2,1)} %get-tuple-element.15.refs_0_, f32[320,432]{1,0:T(8,128)} %get-tuple-element.16.refs_1_, f32[320,432]{1,0:T(8,128)} %get-tuple-element.17.refs_2_, ...), custom_call_target="tpu_custom_call" | custom-call | tf_op jit(solution)/shard_map/write/pallas_call | solution.py:805

commit v4 on v3

--- a/solution.py
+++ b/solution.py
@@ -41,7 +41,7 @@
     x_ref, dy_ref, gain_ref, gate_ref, up_ref, down_ref, in_sem,
     dx_ref, gate_grad, up_grad, down_grad, gain_grad, out_sem,
     x_all, dy_all, n_all, w_all, w_t, dx_t, gain_col, gu, fac, hid, act, d_hid, scale, stat,
-    zs, zr, xls, xlr, ahs, ahr, afs, afr, bxs, bxr, bhs, bhr, bfs, bfr, axs, axr, ggs, ggr,
+    zs, zr, xls, xlr, ahs, ahr, afs, afr, bxs, bxr, bhs, bhr, bfs, bfr, axs, axr, own, ggs, ggr,
     xs_sem, xr_sem, ts_sem, tr_sem, ws_sem, wr_sem, zs_sem, zr_sem, gs_sem, gr_sem, hs_sem, hr_sem, cs_sem, cr_sem, go_sem,
 ):
     s = lax.axis_index("section")
@@ -254,12 +254,12 @@
         ring_t.paired()
         halves[0].near()
         ring_x.step(1)
-        halves[1].near()
         ring_t.step(0)
         ring_x.step(2)
-        halves[0].next()
+        halves[1].near()
         ring_t.step(1)
         go(0)
+        halves[0].next()
         ring_x.step(3)
 
     @pl.when(s == 0)
@@ -270,14 +270,14 @@
         ring_x.begin_z()
         ring_x.paired()
         ring_x.step(0)
-        ring_x.step(1)
         pl.semaphore_wait(go_sem.at[1], 1)
         for one in halves:
             one.begin()
+        ring_x.step(1)
         ring_x.step(2)
+        halves[0].near()
         ring_x.step(3)
-        for one in halves:
-            one.near()
+        halves[1].near()
         halves[0].next()
 
     def wide(narrow):
@@ -314,6 +314,7 @@
     @pl.when(s == 1)
     def _():
         ring_t.step(2)
+        go(1)
 
     for way in WAYS:
         for one in halves:
@@ -325,10 +326,6 @@
 
     for one in halves:
         one.end()
-
-    @pl.when(s == 1)
-    def _():
-        go(1)
 
     gate_up(y + 2, False)
 
@@ -501,7 +498,7 @@
 
     class Grads:
         def __init__(self, p):
-            self.p, self.first, self.send = p, 13 * p, gs_sem.at[p]
+            self.p, self.first, self.send = p, 15 * p, gs_sem.at[p]
             self.start, self.width = LANES[p]
             self.lanes = pl.ds(self.start, self.width)
 
@@ -523,9 +520,13 @@
         def a_half(self, way):
             return self.copy(ahs, ahr, (self.all(2), h_rows[way](AH)), 0 if way > 0 else 1, y_dev[way])
 
+        def a_rest(self, way):
+            i = 0 if way > 0 else 1
+            return self.copy(afs, afr, (i, self.all(2), h_rows[-way](AH)), 2 + i, y_dev[way])
+
         def a_full(self, way):
             i = 0 if way > 0 else 1
-            return self.copy(afs, afr, (i, self.all(2), self.all(PA)), 2 + i, y_dev[way])
+            return self.copy(afs, afr, (i, self.all(2), h_rows[way](AH)), 13 + i, y_dev[way])
 
         def b_over(self, o):
             return self.copy(bxs, bxr, (o, self.all(PB)), 4 + o, x_dev)
@@ -547,25 +548,26 @@
                 self.a_half(way).start()
             self.send_over(2)
 
+        def begin_rest(self):
+            for i, way in enumerate(WAYS):
+                for n in (0, 1):
+                    value = self.part(at_y(way, n == 1), A_ROWS)
+                    own[i, n, :, self.lanes] = value[:AH] if way > 0 else value[AH:]
+                    rest = value[AH:] if way > 0 else value[:AH]
+                    afs[i, n, h_rows[-way](AH), self.lanes] = rest.astype(BF16)
+                self.a_rest(way).start()
+
         def send_over(self, o):
             bxs[o, :, self.lanes] = self.part(at_y(o, True), B_ROWS).astype(BF16)
             self.b_over(o).start()
-
-        def rest(self):
-            for o in (1, 3, 0):
-                self.send_over(o)
 
         def a_next(self):
             for i, way in enumerate(WAYS):
                 self.a_half(way).wait_recv()
                 rows = h_rows[way](AH)
-                other = h_rows[-way](AH)
                 for n in (0, 1):
-                    value = self.part(at_y(way, n == 1), A_ROWS)
-                    mine = value[:AH] if way > 0 else value[AH:]
-                    rest = value[AH:] if way > 0 else value[:AH]
-                    afs[i, n, rows, self.lanes] = (mine + ahr[n, rows, self.lanes].astype(F32)).astype(BF16)
-                    afs[i, n, other, self.lanes] = rest.astype(BF16)
+                    value = own[i, n, :, self.lanes] + ahr[n, rows, self.lanes].astype(F32)
+                    afs[i, n, rows, self.lanes] = value.astype(BF16)
                 self.a_full(way).start()
 
         def crossed(self, o):
@@ -597,6 +599,7 @@
 
         def a_last(self):
             for way in WAYS:
+                self.a_rest(way).wait_recv()
                 self.a_full(way).wait_recv()
             axs[:, self.lanes] = self.a_sum(1).astype(BF16)
             self.a_over().start()
@@ -616,12 +619,6 @@
             copy(block, block, self.send, gr_sem, 0, x_dev).wait_send()
 
     grads = [Grads(p) for p in range(len(LANES))]
-
-    def grads_begin():
-        for one in grads:
-            one.begin()
-        for one in grads:
-            one.rest()
 
     def unpack(rows, p, value, add=False):
         def put(ref, lanes, part):
@@ -636,6 +633,18 @@
             put(down_grad, slice(0, MAIN + TAIL), value[:, 128 : 128 + MAIN + TAIL])
 
     top, rest = slice(0, PA), slice(PA, FS)
+
+    def grads_begin(between):
+        for one in grads:
+            one.begin()
+        between()
+        grads[0].send_over(1)
+        grads[0].send_over(3)
+        grads[0].begin_rest()
+        grads[0].send_over(0)
+        for o in (1, 3, 0):
+            grads[1].send_over(o)
+        grads[1].begin_rest()
 
     @pl.when(s == 1)
     def _():
@@ -646,10 +655,7 @@
             for one in handed(q):
                 one.start()
         send_gain(terms)
-        for one in grads:
-            one.begin()
-        for one in grads:
-            one.rest()
+        grads_begin(lambda: None)
         for one in grads:
             one.b_next()
             one.a_next()
@@ -662,26 +668,22 @@
 
     @pl.when(s == 0)
     def _():
-        grads[0].begin()
-        z_step(0)
-        grads[1].begin()
-        for one in grads:
-            one.rest()
+        grads_begin(lambda: z_step(0))
+        grads[0].b_next()
         z_step(1)
-        grads[0].b_next()
         grads[0].a_next()
-        z_step(2)
         grads[1].b_next()
         grads[1].a_next()
+        z_step(2)
         grads[0].b_last()
         z_step(3)
         grads[0].a_last()
+        grads[1].b_last()
         unpack(top, 0, grads[0].a_sum(0))
-        grads[1].b_last()
+        unpack(rest, 0, grads[0].crossed(0))
+        grads[1].a_last()
         ended = z_end()
-        unpack(rest, 0, grads[0].crossed(0))
         unpack(rest, 1, grads[1].crossed(0))
-        grads[1].a_last()
         send_gain(finish(*ended))
         unpack(top, 1, grads[1].a_sum(0))
 
@@ -792,10 +794,11 @@
             *(pltpu.VMEM((PB, PW), BF16),) * 2,
             *(pltpu.VMEM((2, PB, PW), BF16),) * 2,
             *(pltpu.VMEM((PA, PW), BF16),) * 2,
+            pltpu.VMEM((2, 2, PA // 2, PW), F32),
             pltpu.VMEM((8, LW), F32),
             pltpu.VMEM((7, 8, LW), F32),
             dma, ring, dma, ring, dma((2,)), dma((24,)),
-            dma, ring, dma((2,)), dma((26,)), dma((7,)), dma((7,)), dma((4 * PIECES,)), dma((PIECES,)),
+            dma, ring, dma((2,)), dma((30,)), dma((7,)), dma((7,)), dma((4 * PIECES,)), dma((PIECES,)),
             pltpu.SemaphoreType.REGULAR((2,)),
         ],
         compiler_params=pltpu.CompilerParams(

time: 133 us -> 134 us (level)
  Pallas kernels: 131 us -> 133 us
    pallas_call x1, Pallas kernels: 129 us -> 130 us  [window(): pl.pallas_call(kernel, name='window', out_shape=shapes, in_specs=[hbm] *...]
where the time goes in v4:
time: 134 us
  Pallas kernels  133 us (99%)
    pallas_call x1, Pallas kernels, window(): pl.pallas_call(kernel, name='window', out_shape=shapes, in_specs=[hbm] *...  130 us

profile of v4, /device:TPU:8, one launch (start us, length us, event | category | flops | bytes accessed | tf_op | source)
XLA Modules:
  0.0 133.7 jit_solution(5652400297707414817)
XLA Ops:
  0.6 130.3 %window.1 = (bf16[512,160]{1,0:T(8,128)(2,1)}, f32[320,432]{1,0:T(8,128)}, f32[320,432]{1,0:T(8,128)}, f32[320,432]{1,0:T(8,128)}, f32[1,160]{1,0:T(1,128)}) custom-call(bf16[512,160]{1,0:T(8,128)(2,1)} %bitcast.16, bf16[512,160]{1,0:T(8,128)(2,1)} %bitcast.17, f32[1,2560]{1,0:T(1,128)} %gain_in.1, bf16[320,432]{1,0:T(8,128)(2,1)} %bitcast.13, ...), custom_call_target="tpu_custom_call" | custom-call | tf_op jit(solution)/shard_map/window/pallas_call | solution.py:762
  131.0 2.5 %write.1 = (bf16[512,160]{1,0:T(8,128)(2,1)}, f32[320,432]{1,0:T(8,128)}, f32[320,432]{1,0:T(8,128)}, f32[320,432]{1,0:T(8,128)}, f32[1,160]{1,0:T(1,128)}) custom-call(bf16[512,160]{1,0:T(8,128)(2,1)} %get-tuple-element.15.refs_0_, f32[320,432]{1,0:T(8,128)} %get-tuple-element.16.refs_1_, f32[320,432]{1,0:T(8,128)} %get-tuple-element.17.refs_2_, ...), custom_call_target="tpu_custom_call" | custom-call | tf_op jit(solution)/shard_map/write/pallas_call | solution.py:808

commit v5 on v4

--- a/solution.py
+++ b/solution.py
@@ -1,3 +1,5 @@
+import functools
+
 import jax
 import jax.numpy as jnp
 from jax import lax
@@ -6,6 +8,7 @@
 from jax.sharding import PartitionSpec as P
 
 EPSILON = 1e-05
+SPAN = 1000
 MESH = pl.DeviceIdType.MESH
 F32, BF16 = jnp.float32, jnp.bfloat16
 
@@ -26,6 +29,27 @@
 WAYS = (1, -1)
 LANES = ((0, 2 * MAIN), (2 * MAIN, PW - 2 * MAIN))
 
+ORDER = (
+    (
+        "w1", "Xb", "w0", "Xz", "Wb0", "Xp", "X0.0", "Wn-0", "X0.1", "X1.0", "Wo0", "Wn+0", "Wm0", "Wb1",
+        "Wn-1", "X2.0", "Wf+0", "cols", "Wo1", "X1.1", "X2.1", "X3.0", "Tp", "Wm1", "Wf+1", "Wf-1", "T0.0",
+        "Wn+1", "X3.1", "Wf-0", "T0.1", "N", "T1.0", "GU0", "T1.1", "GU+", "T2.0", "GU-", "T2.1", "GU2",
+        "T3.0", "dH0", "T3.1", "dH1", "ah0", "z0", "bx21", "bx20", "z1a", "ah1", "ar+0", "bx01", "z1b", "bn1",
+        "bx30", "ar-0", "bx31", "z2a", "an-0", "z2b", "an+0", "bx11", "bx00", "ub1", "bn0", "z3a", "ar+1",
+        "ar-1", "z3b", "bx10", "ze1", "an-1", "an+1", "bl-1", "bl+1", "bl-0", "ze0", "al0", "ub0", "bl+0",
+        "ua0", "fin", "gain", "al1", "fb1", "fb0", "ua1", "fa0", "fa1",
+    ),
+    (
+        "Xb", "Tb", "Xz", "Wb0", "cols", "Tz", "Xp", "Wb1", "X0.0", "X0.1", "Wn+0", "Wn-0", "go0", "Tp",
+        "X1.0", "X1.1", "Wn-1", "Wo0", "T0.0", "X2.0", "Wn+1", "X2.1", "T0.1", "Wm1", "Wo1", "Wm0", "Wf+0",
+        "T1.0", "Wf-0", "X3.0", "X3.1", "N", "go1", "T1.1", "Wf-1", "Wf+1", "GU0", "T2.0", "GU+", "T2.1",
+        "GU-", "T3.0", "GU2", "dH0", "T3.1", "dH1", "z0", "z1a", "bx21", "bx20", "ah0", "bx30", "z1b", "ar-0",
+        "z2a", "z2b", "ar+0", "z3a", "z3b", "an-0", "ze1", "bn1", "ah1", "an+0", "ar-1", "ze0", "fin", "bx01",
+        "an-1", "bn0", "bx11", "ar+1", "bx00", "an+1", "ub1", "bx10", "gain", "bl+1", "bx31", "al0", "bl-0",
+        "bl+0", "bl-1", "al1", "ub0", "fb0", "ua0", "ua1", "fa0", "fb1", "fa1",
+    ),
+)
+
 
 def dot(a, b):
     return lax.dot_general(a, b, (((1,), (0,)), ((), ())), preferred_element_type=F32)
@@ -40,7 +64,7 @@
     dx_out, gate_out, up_out, down_out, gain_out,
     x_ref, dy_ref, gain_ref, gate_ref, up_ref, down_ref, in_sem,
     dx_ref, gate_grad, up_grad, down_grad, gain_grad, out_sem,
-    x_all, dy_all, n_all, w_all, w_t, dx_t, gain_col, gu, fac, hid, act, d_hid, scale, stat,
+    x_all, dy_all, n_all, w_all, w_t, dx_t, gain_col, gu, fac, hid, act, d_hid, scale, stat, ring_sum, ring_stat,
     zs, zr, xls, xlr, ahs, ahr, afs, afr, bxs, bxr, bhs, bhr, bfs, bfr, axs, axr, own, ggs, ggr,
     xs_sem, xr_sem, ts_sem, tr_sem, ws_sem, wr_sem, zs_sem, zr_sem, gs_sem, gr_sem, hs_sem, hr_sem, cs_sem, cr_sem, go_sem,
 ):
@@ -148,14 +172,13 @@
                 self.out(1, 0, 1, q).start()
                 self.out(-1, 0, 1, q).start()
 
-        def step(self, k):
-            for j in (0, 1):
-                for q in range(PIECES):
-                    for way in (1, -1):
-                        if self.sends(way, k, j):
-                            self.into(way, k, j, q).wait_recv()
-                            if k < 3 and self.sends(way, k + 1, j):
-                                self.out(way, k + 1, j, q).start()
+        def step(self, k, j):
+            for q in range(PIECES):
+                for way in (1, -1):
+                    if self.sends(way, k, j):
+                        self.into(way, k, j, q).wait_recv()
+                        if k < 3 and self.sends(way, k + 1, j):
+                            self.out(way, k + 1, j, q).start()
 
         def drain(self, blocks):
             block = self.whole.at[pl.ds(0, blocks * LW)]
@@ -199,21 +222,24 @@
             for way in WAYS:
                 self.full(way).start()
 
-        def near(self):
-            for i, way in enumerate(WAYS):
-                self.full(way, 1).wait_recv()
-                self.half(way).start()
-                self.late(i).start()
+        def near(self, way):
+            i = 0 if way > 0 else 1
+            self.full(way, 1).wait_recv()
+            self.half(way).start()
+            self.late(i).start()
+
+        def beside(self):
             self.over(True).wait_recv()
             for way in WAYS:
                 self.far(way).start()
 
-        def next(self):
+        def middle(self):
             self.half(-1, 2).wait_recv()
             self.late(2).start()
-            for way in WAYS:
-                self.far(way, 1).wait_recv()
-                self.far_half(way).start()
+
+        def next(self, way):
+            self.far(way, 1).wait_recv()
+            self.far_half(way).start()
 
         def side(self, way):
             self.late(0 if way > 0 else 1, True).wait_recv()
@@ -240,61 +266,25 @@
     def go(i):
         pl.semaphore_signal(go_sem.at[i], inc=1, device_id=core_dev, device_id_type=MESH)
 
-    @pl.when(s == 1)
-    def _():
-        ring_x.begin()
-        ring_x.begin_z()
-        halves[0].begin()
-        ring_t.begin()
-        halves[1].begin()
-        columns()
-        ring_x.paired()
-        ring_x.step(0)
-        ring_t.begin_z()
-        ring_t.paired()
-        halves[0].near()
-        ring_x.step(1)
-        ring_t.step(0)
-        ring_x.step(2)
-        halves[1].near()
-        ring_t.step(1)
-        go(0)
-        halves[0].next()
-        ring_x.step(3)
-
-    @pl.when(s == 0)
-    def _():
-        ring_x.begin()
-        columns()
-        pl.semaphore_wait(go_sem.at[0], 1)
-        ring_x.begin_z()
-        ring_x.paired()
-        ring_x.step(0)
-        pl.semaphore_wait(go_sem.at[1], 1)
-        for one in halves:
-            one.begin()
-        ring_x.step(1)
-        ring_x.step(2)
-        halves[0].near()
-        ring_x.step(3)
-        halves[1].near()
-        halves[0].next()
+    def wait_go(i):
+        pl.semaphore_wait(go_sem.at[i], 1)
 
     def wide(narrow):
         return jnp.concatenate([narrow] * (TOK // 128), axis=1)
 
-    def square(i, total):
-        block = x_all[t_rows(i), :].astype(F32)
-        return total + jnp.sum(block * block, axis=0, keepdims=True)
-
-    total = lax.fori_loop(0, 16, square, jnp.zeros((1, TOK), F32))
-    scale[...] = lax.rsqrt(total / DM + EPSILON)
-
-    @pl.loop(0, 16)
-    def _(i):
-        rows = t_rows(i)
-        unit = x_all[rows, :].astype(F32) * scale[...]
-        n_all[rows, :] = (unit * wide(gain_col[rows, :])).astype(BF16)
+    def normalize():
+        def square(i, total):
+            block = x_all[t_rows(i), :].astype(F32)
+            return total + jnp.sum(block * block, axis=0, keepdims=True)
+
+        total = lax.fori_loop(0, 16, square, jnp.zeros((1, TOK), F32))
+        scale[...] = lax.rsqrt(total / DM + EPSILON)
+
+        @pl.loop(0, 16)
+        def _(i):
+            rows = t_rows(i)
+            unit = x_all[rows, :].astype(F32) * scale[...]
+            n_all[rows, :] = (unit * wide(gain_col[rows, :])).astype(BF16)
 
     def gate_up(block, first):
         cols = pl.ds(pl.multiple_of(lax.rem(block, Y_RING) * 2 * FS, 128), 2 * FS)
@@ -307,27 +297,6 @@
             rows = pl.ds(pl.multiple_of(i * (GU // 2), 64), GU // 2)
             value = dot(w_t[rows, cols], n_all[cols, :])
             gu[rows, :] = value if first else gu[rows, :] + value
-
-    halves[1].next()
-    gate_up(y, True)
-
-    @pl.when(s == 1)
-    def _():
-        ring_t.step(2)
-        go(1)
-
-    for way in WAYS:
-        for one in halves:
-            one.side(way)
-
-    @pl.loop(0, 2)
-    def _(i):
-        gate_up(y + 1 + 2 * i, False)
-
-    for one in halves:
-        one.end()
-
-    gate_up(y + 2, False)
 
     spans = ((0, MAIN, MAIN, 0), (2 * MAIN, 2 * MAIN + TAIL, TAIL, MAIN))
 
@@ -339,10 +308,11 @@
         fac[gate_at : gate_at + size, :] = up * sig * (1.0 + gate * (1.0 - sig))
         fac[up_at : up_at + size, :] = silu
 
-    for span in spans:
-        factors(*span)
-    hid[MAIN + TAIL :, :] = jnp.zeros((DN - MAIN - TAIL, TOK), BF16)
-    act[GU - 32 :, :] = jnp.zeros((32, TOK), BF16)
+    def all_factors():
+        for span in spans:
+            factors(*span)
+        hid[MAIN + TAIL :, :] = jnp.zeros((DN - MAIN - TAIL, TOK), BF16)
+        act[GU - 32 :, :] = jnp.zeros((32, TOK), BF16)
 
     def handed(q):
         rows = t_rows(t, q * PR, PR)
@@ -356,26 +326,16 @@
             ))
         return made
 
-    @pl.when(s == 0)
-    def _():
-        ring_t.paired()
-        for q in range(PIECES):
-            handed(q)[0].wait_recv()
-        for k in range(3):
-            ring_t.step(k)
-
     def hidden_back(block):
         cols = pl.ds(pl.multiple_of(lax.rem(block, Z_RING // 2) * 4 * LW, 128), 4 * LW)
         return dot(w_t[GU:, cols], dy_all[cols, :])
 
-    d_hid[...] = hidden_back(lax.div(z, 2))
-
-    @pl.loop(0, 2)
-    def _(i):
-        d_hid[...] += hidden_back(lax.div(z, 2) + 1 + 2 * i)
-
-    ring_t.step(3)
-    d_hid[...] += hidden_back(lax.div(z, 2) + 2)
+    def back_first():
+        d_hid[...] = hidden_back(lax.div(z, 2))
+
+        @pl.loop(0, 2)
+        def _(i):
+            d_hid[...] += hidden_back(lax.div(z, 2) + 1 + 2 * i)
 
     def back(gate_at, up_at, size, at):
         grad = d_hid[at : at + size, :]
@@ -389,7 +349,9 @@
             axis=0, keepdims=True,
         )
 
-    stat[...] = back(*spans[0]) + back(*spans[1])
+    def back_last():
+        d_hid[...] += hidden_back(lax.div(z, 2) + 2)
+        stat[...] = back(*spans[0]) + back(*spans[1])
 
     def partial(off, j):
         rows = t_rows(at_z(off, j == 1))
@@ -421,8 +383,8 @@
         part = pl.ds(rows.start, rows.stop - rows.start)
         return copy(zs.at[i, part], zr.at[i, part], zs_sem, zr_sem, i * PIECES + q, z_dev[way])
 
-    def z_step(k):
-        for j, way in ((1, 1), (0, -1), (1, -1), (0, 1)) if k < 2 else ((1, 1), (1, -1), (0, 1), (0, -1)):
+    def z_step(k, pairs):
+        for j, way in pairs:
             if not z_has(way, k, j):
                 continue
             value = partial(way * (4 - k), j)
@@ -446,7 +408,7 @@
         rows = pl.ds(q * PR, PR) if q < PIECES else pl.ds(LW, STAT)
         return copy(xls.at[rows], xlr.at[rows], zs_sem, zr_sem, 16 * PIECES + q, l_dev)
 
-    def z_end():
+    def z_end_pair():
         value = partial(0, 1)
         for q in range(PIECES):
             rows = slice(q * PR, (q + 1) * PR)
@@ -456,6 +418,8 @@
                 part = part + zr[z_at(way, 3, 1), rows, :].astype(F32)
             xls[rows, :] = part.astype(BF16)
             to_pair(q).start()
+
+    def z_end():
         value = partial(0, 0)
         total = stat[...]
         for way in WAYS:
@@ -466,20 +430,21 @@
             total = total + stat_of(zr[i, LW:, :])
         xls[LW:, :] = stat_rows(total)
         to_pair(PIECES).start()
-        return value, total
-
-    def finish(value, total):
+        ring_sum[...] = value
+        ring_stat[...] = total
+
+    def finish():
         for q in range(PIECES + 1):
             to_pair(q).wait_recv()
-        d_norm = value + xlr[:LW, :].astype(F32)
-        norm_stat = (total + stat_of(xlr[LW:, :])) / DM
+        d_norm = ring_sum[...] + xlr[:LW, :].astype(F32)
+        norm_stat = (ring_stat[...] + stat_of(xlr[LW:, :])) / DM
         mine = t_rows(t)
         unit = x_all[mine, :].astype(F32) * scale[...]
         dx_t[...] = (
             dy_all[mine, :].astype(F32)
             + scale[...] * (d_norm * wide(gain_col[mine, :]) - unit * norm_stat)
         ).astype(BF16)
-        return d_norm * unit
+        ring_sum[...] = d_norm * unit
 
     gains = [copy(ggs, ggr.at[i], hs_sem.at[i], hr_sem, i, f_devs[i]) for i in range(7)]
 
@@ -546,29 +511,28 @@
                 ahs[n, :, self.lanes] = self.part(at_y(2, n == 1), A_ROWS).astype(BF16)
             for way in WAYS:
                 self.a_half(way).start()
-            self.send_over(2)
-
-        def begin_rest(self):
-            for i, way in enumerate(WAYS):
-                for n in (0, 1):
-                    value = self.part(at_y(way, n == 1), A_ROWS)
-                    own[i, n, :, self.lanes] = value[:AH] if way > 0 else value[AH:]
-                    rest = value[AH:] if way > 0 else value[:AH]
-                    afs[i, n, h_rows[-way](AH), self.lanes] = rest.astype(BF16)
-                self.a_rest(way).start()
+
+        def begin_rest(self, way):
+            i = 0 if way > 0 else 1
+            for n in (0, 1):
+                value = self.part(at_y(way, n == 1), A_ROWS)
+                own[i, n, :, self.lanes] = value[:AH] if way > 0 else value[AH:]
+                rest = value[AH:] if way > 0 else value[:AH]
+                afs[i, n, h_rows[-way](AH), self.lanes] = rest.astype(BF16)
+            self.a_rest(way).start()
 
         def send_over(self, o):
             bxs[o, :, self.lanes] = self.part(at_y(o, True), B_ROWS).astype(BF16)
             self.b_over(o).start()
 
-        def a_next(self):
-            for i, way in enumerate(WAYS):
-                self.a_half(way).wait_recv()
-                rows = h_rows[way](AH)
-                for n in (0, 1):
-                    value = own[i, n, :, self.lanes] + ahr[n, rows, self.lanes].astype(F32)
-                    afs[i, n, rows, self.lanes] = value.astype(BF16)
-                self.a_full(way).start()
+        def a_next(self, way):
+            i = 0 if way > 0 else 1
+            self.a_half(way).wait_recv()
+            rows = h_rows[way](AH)
+            for n in (0, 1):
+                value = own[i, n, :, self.lanes] + ahr[n, rows, self.lanes].astype(F32)
+                afs[i, n, rows, self.lanes] = value.astype(BF16)
+            self.a_full(way).start()
 
         def crossed(self, o):
             self.b_over(o).wait_recv()
@@ -579,17 +543,17 @@
             for way in WAYS:
                 self.b_half(way).start()
 
-        def b_last(self):
-            for i, way in enumerate(WAYS):
-                value = self.crossed(1 if way > 0 else 3)
-                self.b_half(way).wait_recv()
-                rows = h_rows[way](BH)
-                other = h_rows[-way](BH)
-                mine = value[:BH] if way > 0 else value[BH:]
-                rest = value[BH:] if way > 0 else value[:BH]
-                bfs[i, rows, self.lanes] = (mine + bhr[rows, self.lanes].astype(F32)).astype(BF16)
-                bfs[i, other, self.lanes] = rest.astype(BF16)
-                self.b_full(way).start()
+        def b_last(self, way):
+            i = 0 if way > 0 else 1
+            value = self.crossed(1 if way > 0 else 3)
+            self.b_half(way).wait_recv()
+            rows = h_rows[way](BH)
+            other = h_rows[-way](BH)
+            mine = value[:BH] if way > 0 else value[BH:]
+            rest = value[BH:] if way > 0 else value[:BH]
+            bfs[i, rows, self.lanes] = (mine + bhr[rows, self.lanes].astype(F32)).astype(BF16)
+            bfs[i, other, self.lanes] = rest.astype(BF16)
+            self.b_full(way).start()
 
         def a_sum(self, n):
             return (
@@ -633,72 +597,88 @@
             put(down_grad, slice(0, MAIN + TAIL), value[:, 128 : 128 + MAIN + TAIL])
 
     top, rest = slice(0, PA), slice(PA, FS)
-
-    def grads_begin(between):
-        for one in grads:
-            one.begin()
-        between()
-        grads[0].send_over(1)
-        grads[0].send_over(3)
-        grads[0].begin_rest()
-        grads[0].send_over(0)
-        for o in (1, 3, 0):
-            grads[1].send_over(o)
-        grads[1].begin_rest()
-
-    @pl.when(s == 1)
-    def _():
-        for k in range(4):
-            z_step(k)
-        terms = finish(*z_end())
-        for q in range(PIECES):
-            for one in handed(q):
-                one.start()
-        send_gain(terms)
-        grads_begin(lambda: None)
-        for one in grads:
-            one.b_next()
-            one.a_next()
-        for p, one in enumerate(grads):
-            one.b_last()
-            unpack(rest, p, one.crossed(0))
-        for p, one in enumerate(grads):
-            one.a_last()
-            unpack(top, p, one.a_sum(0))
-
-    @pl.when(s == 0)
-    def _():
-        grads_begin(lambda: z_step(0))
-        grads[0].b_next()
-        z_step(1)
-        grads[0].a_next()
-        grads[1].b_next()
-        grads[1].a_next()
-        z_step(2)
-        grads[0].b_last()
-        z_step(3)
-        grads[0].a_last()
-        grads[1].b_last()
-        unpack(top, 0, grads[0].a_sum(0))
-        unpack(rest, 0, grads[0].crossed(0))
-        grads[1].a_last()
-        ended = z_end()
-        unpack(rest, 1, grads[1].crossed(0))
-        send_gain(finish(*ended))
-        unpack(top, 1, grads[1].a_sum(0))
-
-    dx_ref[...] = dx_t[...].T
     writes = [
         pltpu.make_async_copy(src, dst, out_sem.at[i])
         for i, (src, dst) in enumerate((
             (dx_ref, dx_out), (gate_grad, gate_out), (up_grad, up_out), (down_grad, down_out), (gain_grad, gain_out),
         ))
     ]
-    writes[0].start()
-
-    for p, one in enumerate(grads):
-        unpack(top, p, one.arrived_a(), True)
-        unpack(rest, p, one.arrived_b(), True)
+
+    def program(section, start):
+        ops = {"cols": columns, "N": normalize}
+        for name, ring in (("X", ring_x), ("T", ring_t)):
+            ops[name + "b"], ops[name + "z"], ops[name + "p"] = ring.begin, ring.begin_z, ring.paired
+            for k in range(4):
+                for j in (0, 1):
+                    ops[f"{name}{k}.{j}"] = functools.partial(ring.step, k, j)
+        for i in (0, 1):
+            ops[f"go{i}"] = functools.partial(go, i)
+            ops[f"w{i}"] = functools.partial(wait_go, i)
+        for p, one in enumerate(halves):
+            ops[f"Wb{p}"], ops[f"Wo{p}"], ops[f"Wm{p}"] = one.begin, one.beside, one.middle
+            for way, sign in zip(WAYS, "+-"):
+                ops[f"Wn{sign}{p}"] = functools.partial(one.near, way)
+                ops[f"Wf{sign}{p}"] = functools.partial(one.next, way)
+
+        def side(way):
+            for one in halves:
+                one.side(way)
+            gate_up(y - way + Y_RING, False)
+
+        def last():
+            for one in halves:
+                one.end()
+            gate_up(y + 2, False)
+            all_factors()
+
+        def hidden():
+            if section == 0:
+                for q in range(PIECES):
+                    handed(q)[0].wait_recv()
+            back_first()
+
+        def done():
+            finish()
+            if section == 1:
+                for q in range(PIECES):
+                    for one in handed(q):
+                        one.start()
+
+        def gain():
+            send_gain(ring_sum[...])
+            dx_ref[...] = dx_t[...].T
+            writes[0].start()
+
+        ops["GU0"] = functools.partial(gate_up, y, True)
+        ops["GU+"], ops["GU-"] = functools.partial(side, 1), functools.partial(side, -1)
+        ops["GU2"], ops["dH0"], ops["dH1"] = last, hidden, back_last
+        ops["z0"] = functools.partial(z_step, 0, ((0, 1), (1, -1)))
+        ops["z1a"] = functools.partial(z_step, 1, ((1, 1), (0, -1)))
+        ops["z1b"] = functools.partial(z_step, 1, ((1, -1), (0, 1)))
+        for k in (2, 3):
+            ops[f"z{k}a"] = functools.partial(z_step, k, ((1, 1), (1, -1)))
+            ops[f"z{k}b"] = functools.partial(z_step, k, ((0, 1), (0, -1)))
+        ops["ze1"], ops["ze0"], ops["fin"], ops["gain"] = z_end_pair, z_end, done, gain
+        for p, one in enumerate(grads):
+            ops[f"ah{p}"], ops[f"bn{p}"], ops[f"al{p}"] = one.begin, one.b_next, one.a_last
+            for o in range(4):
+                ops[f"bx{o}{p}"] = functools.partial(one.send_over, o)
+            for way, sign in zip(WAYS, "+-"):
+                ops[f"ar{sign}{p}"] = functools.partial(one.begin_rest, way)
+                ops[f"an{sign}{p}"] = functools.partial(one.a_next, way)
+                ops[f"bl{sign}{p}"] = functools.partial(one.b_last, way)
+            ops[f"ub{p}"] = lambda p=p, one=one: unpack(rest, p, one.crossed(0))
+            ops[f"ua{p}"] = lambda p=p, one=one: unpack(top, p, one.a_sum(0))
+            ops[f"fa{p}"] = lambda p=p, one=one: unpack(top, p, one.arrived_a(), True)
+            ops[f"fb{p}"] = lambda p=p, one=one: unpack(rest, p, one.arrived_b(), True)
+        for name in ORDER[section][start : start + SPAN]:
+            with jax.named_scope(name):
+                ops[name]()
+
+    for start in range(0, max(map(len, ORDER)), SPAN):
+        for section in (1, 0):
+            pl.when(s == section)(functools.partial(program, section, start))
+
     summed = ggs[...]
     for i in range(7):
         gains[i].wait_recv()
@@ -784,6 +764,8 @@
             pltpu.VMEM((DN, TOK), F32),
             pltpu.VMEM((1, TOK), F32),
             pltpu.VMEM((1, TOK), F32),
+            pltpu.VMEM((LW, TOK), F32),
+            pltpu.VMEM((1, TOK), F32),
             pltpu.VMEM((16, LW + STAT, TOK), BF16),
             pltpu.VMEM((16, LW + STAT, TOK), BF16),
             pltpu.VMEM((LW + STAT, TOK), BF16),

time: 134 us -> 126 us (0.940)
  Pallas kernels: 133 us -> 125 us
    pallas_call x1, Pallas kernels: 130 us -> 122 us  [window(): pl.pallas_call(kernel, name='window', out_shape=shapes, in_specs=[hbm] *...]
where the time goes in v5:
time: 126 us
  Pallas kernels  125 us (99%)
    pallas_call x1, Pallas kernels, window(): pl.pallas_call(kernel, name='window', out_shape=shapes, in_specs=[hbm] *...  122 us
    pallas_call x1, Pallas kernels, window(): pl.pallas_call(write, name='write', out_shape=shapes, in_specs=[hbm] * 5,...  2.53 us

profile of v5, /device:TPU:8, one launch (start us, length us, event | category | flops | bytes accessed | tf_op | source)
XLA Modules:
  0.0 125.7 jit_solution(1498565654981819388)
XLA Ops:
  0.6 122.3 %window.1 = (bf16[512,160]{1,0:T(8,128)(2,1)}, f32[320,432]{1,0:T(8,128)}, f32[320,432]{1,0:T(8,128)}, f32[320,432]{1,0:T(8,128)}, f32[1,160]{1,0:T(1,128)}) custom-call(bf16[512,160]{1,0:T(8,128)(2,1)} %bitcast.16, bf16[512,160]{1,0:T(8,128)(2,1)} %bitcast.17, f32[1,2560]{1,0:T(1,128)} %gain_in.1, bf16[320,432]{1,0:T(8,128)(2,1)} %bitcast.13, ...), custom_call_target="tpu_custom_call" | custom-call | tf_op jit(solution)/shard_map/window/pallas_call | solution.py:742
  122.9 2.5 %write.1 = (bf16[512,160]{1,0:T(8,128)(2,1)}, f32[320,432]{1,0:T(8,128)}, f32[320,432]{1,0:T(8,128)}, f32[320,432]{1,0:T(8,128)}, f32[1,160]{1,0:T(1,128)}) custom-call(bf16[512,160]{1,0:T(8,128)(2,1)} %get-tuple-element.15.refs_0_, f32[320,432]{1,0:T(8,128)} %get-tuple-element.16.refs_1_, f32[320,432]{1,0:T(8,128)} %get-tuple-element.17.refs_2_, ...), custom_call_target="tpu_custom_call" | custom-call | tf_op jit(solution)/shard_map/write/pallas_call | solution.py:790

commit v6 on v5

--- a/solution.py
+++ b/solution.py
@@ -8,7 +8,6 @@
 from jax.sharding import PartitionSpec as P
 
 EPSILON = 1e-05
-SPAN = 1000
 MESH = pl.DeviceIdType.MESH
 F32, BF16 = jnp.float32, jnp.bfloat16
 
@@ -31,22 +30,23 @@
 
 ORDER = (
     (
-        "w1", "Xb", "w0", "Xz", "Wb0", "Xp", "X0.0", "Wn-0", "X0.1", "X1.0", "Wo0", "Wn+0", "Wm0", "Wb1",
-        "Wn-1", "X2.0", "Wf+0", "cols", "Wo1", "X1.1", "X2.1", "X3.0", "Tp", "Wm1", "Wf+1", "Wf-1", "T0.0",
-        "Wn+1", "X3.1", "Wf-0", "T0.1", "N", "T1.0", "GU0", "T1.1", "GU+", "T2.0", "GU-", "T2.1", "GU2",
-        "T3.0", "dH0", "T3.1", "dH1", "ah0", "z0", "bx21", "bx20", "z1a", "ah1", "ar+0", "bx01", "z1b", "bn1",
-        "bx30", "ar-0", "bx31", "z2a", "an-0", "z2b", "an+0", "bx11", "bx00", "ub1", "bn0", "z3a", "ar+1",
-        "ar-1", "z3b", "bx10", "ze1", "an-1", "an+1", "bl-1", "bl+1", "bl-0", "ze0", "al0", "ub0", "bl+0",
-        "ua0", "fin", "gain", "al1", "fb1", "fb0", "ua1", "fa0", "fa1",
+        "w0", "w1", "Xb", "cols", "Xz", "Xp", "Wb0", "X0.0", "X0.1", "Wb1", "Wn-0", "Wo0", "Wm0", "Wo1",
+        "Wn+1", "Wf+0", "Wf+1", "X1.0", "X1.1", "Wn-1", "Wn+0", "X2.0", "Wf-1", "Wf-0", "X2.1", "Tp", "Wm1",
+        "WT0", "T0.0", "X3.0", "WT+", "X3.1", "N", "T0.1", "T1.0", "T1.1", "WT-", "GU0", "WT2", "T2.0", "GU+",
+        "T2.1", "GU-", "dH0", "GU2", "T3.0", "fac", "T3.1", "dH1", "z0", "ah0", "bx21", "z1a", "bx20", "bx10",
+        "ah1", "z1b", "ar+0", "ar-0", "bx00", "bx11", "bn1", "an-0", "z2a", "z2b", "an+0", "ar+1", "bx01",
+        "bn0", "ub0", "z3a", "bx30", "ar-1", "z3b", "an+1", "bx31", "an-1", "ze1", "bl-0", "ze0", "al0",
+        "bl+0", "bl+1", "bl-1", "ua0", "ub1", "al1", "fin", "gain", "fb1", "ua1", "fb0", "fa0", "fa1",
     ),
     (
-        "Xb", "Tb", "Xz", "Wb0", "cols", "Tz", "Xp", "Wb1", "X0.0", "X0.1", "Wn+0", "Wn-0", "go0", "Tp",
-        "X1.0", "X1.1", "Wn-1", "Wo0", "T0.0", "X2.0", "Wn+1", "X2.1", "T0.1", "Wm1", "Wo1", "Wm0", "Wf+0",
-        "T1.0", "Wf-0", "X3.0", "X3.1", "N", "go1", "T1.1", "Wf-1", "Wf+1", "GU0", "T2.0", "GU+", "T2.1",
-        "GU-", "T3.0", "GU2", "dH0", "T3.1", "dH1", "z0", "z1a", "bx21", "bx20", "ah0", "bx30", "z1b", "ar-0",
-        "z2a", "z2b", "ar+0", "z3a", "z3b", "an-0", "ze1", "bn1", "ah1", "an+0", "ar-1", "ze0", "fin", "bx01",
-        "an-1", "bn0", "bx11", "ar+1", "bx00", "an+1", "ub1", "bx10", "gain", "bl+1", "bx31", "al0", "bl-0",
-        "bl+0", "bl-1", "al1", "ub0", "fb0", "ua0", "ua1", "fa0", "fb1", "fa1",
+        "Xb", "Xz", "Tb", "Tz", "Wb0", "Wb1", "Xp", "Tp", "X0.0", "Wn-0", "X0.1", "Wo0", "T0.0", "X1.0",
+        "X1.1", "Wo1", "Wn-1", "Wn+1", "T0.1", "cols", "Wf+0", "T1.0", "X2.0", "Wn+0", "Wm0", "go0", "Wf-0",
+        "X2.1", "WT0", "T1.1", "Wf+1", "go1", "Wm1", "T2.0", "Wf-1", "X3.0", "WT+", "X3.1", "WT-", "N",
+        "T2.1", "GU0", "GU+", "GU-", "WT2", "GU2", "dH0", "T3.0", "fac", "T3.1", "dH1", "z0", "bx21", "z1a",
+        "ah1", "bx30", "bx00", "z1b", "ar+1", "z2a", "z2b", "z3a", "ar-0", "z3b", "ze1", "bn1", "ah0", "ze0",
+        "ar-1", "fin", "bx20", "ub0", "bx31", "ar+0", "gain", "bx11", "an+1", "an+0", "an-1", "bn0", "bx01",
+        "an-0", "bx10", "al1", "bl-1", "ua1", "ub1", "bl+0", "al0", "bl+1", "bl-0", "ua0", "fb0", "fa1",
+        "fa0", "fb1",
     ),
 )
 
@@ -286,11 +286,17 @@
             unit = x_all[rows, :].astype(F32) * scale[...]
             n_all[rows, :] = (unit * wide(gain_col[rows, :])).astype(BF16)
 
-    def gate_up(block, first):
-        cols = pl.ds(pl.multiple_of(lax.rem(block, Y_RING) * 2 * FS, 128), 2 * FS)
+    def block_cols(block):
+        return pl.ds(pl.multiple_of(lax.rem(block, Y_RING) * 2 * FS, 128), 2 * FS)
+
+    def turn(block):
+        cols = block_cols(block)
         for i in range(PW // 128):
             lanes = slice(i * 128, (i + 1) * 128)
             w_t[lanes, cols] = w_all[cols, lanes].T
+
+    def gate_up(block, first):
+        cols = block_cols(block)
 
         @pl.loop(0, 2)
         def _(i):
@@ -317,11 +323,11 @@
     def handed(q):
         rows = t_rows(t, q * PR, PR)
         part = dx_t.at[pl.ds(q * PR, PR)]
-        made = [copy(part, dy_all.at[rows], cs_sem.at[q], cr_sem, q, core_dev)]
+        made = [copy(part, dy_all.at[rows], cs_sem, cr_sem, q, core_dev)]
         for n, i in enumerate((16, 0, 8)):
             made.append(pltpu.make_async_remote_copy(
                 src_ref=part, dst_ref=dy_all.at[rows],
-                send_sem=cs_sem.at[(n + 1) * PIECES + q], recv_sem=tr_sem.at[i * PIECES + q],
+                send_sem=cs_sem, recv_sem=tr_sem.at[i * PIECES + q],
                 device_id=(cross[2], cross[0], cross[1])[n], device_id_type=MESH,
             ))
         return made
@@ -446,7 +452,7 @@
         ).astype(BF16)
         ring_sum[...] = d_norm * unit
 
-    gains = [copy(ggs, ggr.at[i], hs_sem.at[i], hr_sem, i, f_devs[i]) for i in range(7)]
+    gains = [copy(ggs, ggr.at[i], hs_sem, hr_sem, i, f_devs[i]) for i in range(7)]
 
     def send_gain(terms):
         lanes = terms[:, :128] + terms[:, 128:256] + terms[:, 256:384] + terms[:, 384:]
@@ -604,7 +610,7 @@
         ))
     ]
 
-    def program(section, start):
+    def program(section):
         ops = {"cols": columns, "N": normalize}
         for name, ring in (("X", ring_x), ("T", ring_t)):
             ops[name + "b"], ops[name + "z"], ops[name + "p"] = ring.begin, ring.begin_z, ring.paired
@@ -623,13 +629,12 @@
         def side(way):
             for one in halves:
                 one.side(way)
-            gate_up(y - way + Y_RING, False)
+            turn(y - way + Y_RING)
 
         def last():
             for one in halves:
                 one.end()
-            gate_up(y + 2, False)
-            all_factors()
+            turn(y + 2)
 
         def hidden():
             if section == 0:
@@ -649,9 +654,12 @@
             dx_ref[...] = dx_t[...].T
             writes[0].start()
 
-        ops["GU0"] = functools.partial(gate_up, y, True)
-        ops["GU+"], ops["GU-"] = functools.partial(side, 1), functools.partial(side, -1)
-        ops["GU2"], ops["dH0"], ops["dH1"] = last, hidden, back_last
+        ops["WT0"], ops["WT2"] = functools.partial(turn, y), last
+        ops["GU0"], ops["GU2"] = functools.partial(gate_up, y, True), functools.partial(gate_up, y + 2, False)
+        for way, sign in zip(WAYS, "+-"):
+            ops["WT" + sign] = functools.partial(side, way)
+            ops["GU" + sign] = functools.partial(gate_up, y - way + Y_RING, False)
+        ops["fac"], ops["dH0"], ops["dH1"] = all_factors, hidden, back_last
         ops["z0"] = functools.partial(z_step, 0, ((0, 1), (1, -1)))
         ops["z1a"] = functools.partial(z_step, 1, ((1, 1), (0, -1)))
         ops["z1b"] = functools.partial(z_step, 1, ((1, -1), (0, 1)))
@@ -671,13 +679,12 @@
             ops[f"ua{p}"] = lambda p=p, one=one: unpack(top, p, one.a_sum(0))
             ops[f"fa{p}"] = lambda p=p, one=one: unpack(top, p, one.arrived_a(), True)
             ops[f"fb{p}"] = lambda p=p, one=one: unpack(rest, p, one.arrived_b(), True)
-        for name in ORDER[section][start : start + SPAN]:
+        for name in ORDER[section]:
             with jax.named_scope(name):
                 ops[name]()
 
-    for start in range(0, max(map(len, ORDER)), SPAN):
-        for section in (1, 0):
-            pl.when(s == section)(functools.partial(program, section, start))
+    for section in (1, 0):
+        pl.when(s == section)(functools.partial(program, section))
 
     summed = ggs[...]
     for i in range(7):
@@ -695,15 +702,13 @@
     copy(block, block, zs_sem, zr_sem, 0, l_dev).wait_send()
     for one in grads:
         one.drain()
-    for one in gains:
-        one.wait_send()
+    copy(ggr, ggr, hs_sem, hr_sem, 0, x_dev).wait_send()
 
     @pl.when(s == 1)
     def _():
         ring_t.drain(15)
-        for q in range(PIECES):
-            for one in handed(q):
-                one.wait_send()
+        block = x_all.at[pl.ds(0, 4 * LW)]
+        copy(block, block, cs_sem, cr_sem, 0, core_dev).wait_send()
 
     @pl.when(s == 0)
     def _():
@@ -780,7 +785,7 @@
             pltpu.VMEM((8, LW), F32),
             pltpu.VMEM((7, 8, LW), F32),
             dma, ring, dma, ring, dma((2,)), dma((24,)),
-            dma, ring, dma((2,)), dma((30,)), dma((7,)), dma((7,)), dma((4 * PIECES,)), dma((PIECES,)),
+            dma, ring, dma((2,)), dma((30,)), dma, dma((7,)), dma, dma((PIECES,)),
             pltpu.SemaphoreType.REGULAR((2,)),
         ],
         compiler_params=pltpu.CompilerParams(

time: 126 us -> 124 us (0.984)
  Pallas kernels: 125 us -> 123 us
    pallas_call x1, Pallas kernels: 122 us -> 120 us  [window(): pl.pallas_call(kernel, name='window', out_shape=shapes, in_specs=[hbm] *...]
where the time goes in v6:
time: 124 us
  Pallas kernels  123 us (99%)
    pallas_call x1, Pallas kernels, window(): pl.pallas_call(kernel, name='window', out_shape=shapes, in_specs=[hbm] *...  120 us
    pallas_call x1, Pallas kernels, window(): pl.pallas_call(write, name='write', out_shape=shapes, in_specs=[hbm] * 5,...  2.53 us

profile of v6, /device:TPU:8, one launch (start us, length us, event | category | flops | bytes accessed | tf_op | source)
XLA Modules:
  0.0 123.6 jit_solution(13988189144996469529)
XLA Ops:
  0.6 120.2 %window.1 = (bf16[512,160]{1,0:T(8,128)(2,1)}, f32[320,432]{1,0:T(8,128)}, f32[320,432]{1,0:T(8,128)}, f32[320,432]{1,0:T(8,128)}, f32[1,160]{1,0:T(1,128)}) custom-call(bf16[512,160]{1,0:T(8,128)(2,1)} %bitcast.16, bf16[512,160]{1,0:T(8,128)(2,1)} %bitcast.17, f32[1,2560]{1,0:T(1,128)} %gain_in.1, bf16[320,432]{1,0:T(8,128)(2,1)} %bitcast.13, ...), custom_call_target="tpu_custom_call" | custom-call | tf_op jit(solution)/shard_map/window/pallas_call | solution.py:747
  120.8 2.5 %write.1 = (bf16[512,160]{1,0:T(8,128)(2,1)}, f32[320,432]{1,0:T(8,128)}, f32[320,432]{1,0:T(8,128)}, f32[320,432]{1,0:T(8,128)}, f32[1,160]{1,0:T(1,128)}) custom-call(bf16[512,160]{1,0:T(8,128)(2,1)} %get-tuple-element.15.refs_0_, f32[320,432]{1,0:T(8,128)} %get-tuple-element.16.refs_1_, f32[320,432]{1,0:T(8,128)} %get-tuple-element.17.refs_2_, ...), custom_call_target="tpu_custom_call" | custom-call | tf_op jit(solution)/shard_map/write/pallas_call | solution.py:795

commit v7 on v6

--- a/solution.py
+++ b/solution.py
@@ -17,36 +17,40 @@
 DM = LW * 2 * Z_RING
 FS = 320
 PA = 192
-PB = FS - PA
 MAIN, TAIL = 384, 48
+LEFT = 16
+FP = FS + LEFT
 GU = 2 * MAIN + 128
-DN = 512
-PW = GU + DN
+PW = GU + MAIN
+WT = PW + LEFT
+DH = MAIN + TAIL
+HID = 128 + MAIN + LEFT
 STAT = 16
 PIECES = 2
 PR = LW // PIECES
 WAYS = (1, -1)
 LANES = ((0, 2 * MAIN), (2 * MAIN, PW - 2 * MAIN))
+SHARD = (FP, FS)
 
 ORDER = (
     (
-        "w0", "w1", "Xb", "cols", "Xz", "Xp", "Wb0", "X0.0", "X0.1", "Wb1", "Wn-0", "Wo0", "Wm0", "Wo1",
-        "Wn+1", "Wf+0", "Wf+1", "X1.0", "X1.1", "Wn-1", "Wn+0", "X2.0", "Wf-1", "Wf-0", "X2.1", "Tp", "Wm1",
-        "WT0", "T0.0", "X3.0", "WT+", "X3.1", "N", "T0.1", "T1.0", "T1.1", "WT-", "GU0", "WT2", "T2.0", "GU+",
-        "T2.1", "GU-", "dH0", "GU2", "T3.0", "fac", "T3.1", "dH1", "z0", "ah0", "bx21", "z1a", "bx20", "bx10",
-        "ah1", "z1b", "ar+0", "ar-0", "bx00", "bx11", "bn1", "an-0", "z2a", "z2b", "an+0", "ar+1", "bx01",
-        "bn0", "ub0", "z3a", "bx30", "ar-1", "z3b", "an+1", "bx31", "an-1", "ze1", "bl-0", "ze0", "al0",
-        "bl+0", "bl+1", "bl-1", "ua0", "ub1", "al1", "fin", "gain", "fb1", "ua1", "fb0", "fa0", "fa1",
+        "w0", "w1", "Xb", "cols", "Xz", "Wb0", "Xp", "X0.0", "X0.1", "Wb1", "Wo0", "Wn-0", "Wo1", "Wn+1",
+        "Wn+0", "Wn-1", "Wm0", "X1.0", "X1.1", "X2.0", "WT0", "Wf-1", "Wf+0", "X2.1", "Wf-0", "WT-", "Wm1",
+        "Tp", "Wf+1", "WT+", "T0.0", "X3.0", "X3.1", "N", "T0.1", "T1.0", "GU0", "T1.1", "WT2", "GU-", "GU2",
+        "T2.0", "T2.1", "dH0", "GU+", "fac", "T3.0", "T3.1", "dH1", "z0", "ah0", "bx21", "z1a", "bx11",
+        "bx20", "ah1", "bx10", "z1b", "bx01", "ar+0", "bn1", "ar-0", "z2a", "z2b", "ar+1", "an-0", "ar-1",
+        "bx00", "z3a", "bx30", "an+0", "z3b", "bn0", "an-1", "bx31", "an+1", "ub1", "ze1", "bl+1", "ze0",
+        "ub0", "al0", "bl+0", "bl-1", "bl-0", "fin", "al1", "gain", "ua0", "fb0", "ua1", "fb1", "fa0", "fa1",
     ),
     (
-        "Xb", "Xz", "Tb", "Tz", "Wb0", "Wb1", "Xp", "Tp", "X0.0", "Wn-0", "X0.1", "Wo0", "T0.0", "X1.0",
-        "X1.1", "Wo1", "Wn-1", "Wn+1", "T0.1", "cols", "Wf+0", "T1.0", "X2.0", "Wn+0", "Wm0", "go0", "Wf-0",
-        "X2.1", "WT0", "T1.1", "Wf+1", "go1", "Wm1", "T2.0", "Wf-1", "X3.0", "WT+", "X3.1", "WT-", "N",
-        "T2.1", "GU0", "GU+", "GU-", "WT2", "GU2", "dH0", "T3.0", "fac", "T3.1", "dH1", "z0", "bx21", "z1a",
-        "ah1", "bx30", "bx00", "z1b", "ar+1", "z2a", "z2b", "z3a", "ar-0", "z3b", "ze1", "bn1", "ah0", "ze0",
-        "ar-1", "fin", "bx20", "ub0", "bx31", "ar+0", "gain", "bx11", "an+1", "an+0", "an-1", "bn0", "bx01",
-        "an-0", "bx10", "al1", "bl-1", "ua1", "ub1", "bl+0", "al0", "bl+1", "bl-0", "ua0", "fb0", "fa1",
-        "fa0", "fb1",
+        "Xb", "Xz", "Tb", "Tz", "Wb0", "Xp", "Wb1", "X0.0", "Tp", "cols", "T0.0", "X0.1", "Wn+0", "Wn-0",
+        "Wo0", "T0.1", "Wn-1", "X1.0", "X1.1", "Wo1", "T1.0", "Wn+1", "Wf-0", "Wm1", "T1.1", "X2.0", "WT0",
+        "Wf+0", "X2.1", "go1", "Wm0", "Wf+1", "WT+", "go0", "Wf-1", "T2.0", "WT-", "T2.1", "X3.0", "X3.1",
+        "N", "GU0", "GU-", "WT2", "GU+", "GU2", "T3.0", "dH0", "T3.1", "fac", "dH1", "z0", "ar-0", "z1a",
+        "bx21", "ah1", "bx20", "z1b", "ar+1", "z2a", "z2b", "z3a", "z3b", "ze1", "ze0", "ah0", "fin", "an+1",
+        "ar-1", "bn1", "bx11", "bx30", "bx10", "an-1", "bx31", "bx00", "bx01", "bn0", "ar+0", "an+0", "an-0",
+        "gain", "bl+1", "al1", "bl-0", "bl+0", "al0", "bl-1", "ub0", "ua1", "ua0", "ub1", "fb1", "fa1", "fb0",
+        "fa0",
     ),
 )
 
@@ -64,7 +68,7 @@
     dx_out, gate_out, up_out, down_out, gain_out,
     x_ref, dy_ref, gain_ref, gate_ref, up_ref, down_ref, in_sem,
     dx_ref, gate_grad, up_grad, down_grad, gain_grad, out_sem,
-    x_all, dy_all, n_all, w_all, w_t, dx_t, gain_col, gu, fac, hid, act, d_hid, scale, stat, ring_sum, ring_stat,
+    x_all, dy_all, n_all, w_all, w_t, dx_t, gain_col, gu, fac, hid, act, d_hid, scale, stat, ring_sum, ring_stat, left_sum,
     zs, zr, xls, xlr, ahs, ahr, afs, afr, bxs, bxr, bhs, bhr, bfs, bfr, axs, axr, own, ggs, ggr,
     xs_sem, xr_sem, ts_sem, tr_sem, ws_sem, wr_sem, zs_sem, zr_sem, gs_sem, gr_sem, hs_sem, hr_sem, cs_sem, cr_sem, go_sem,
 ):
@@ -91,6 +95,9 @@
 
     def f_rows(index, start=0, size=FS):
         return pl.ds(pl.multiple_of(index * FS + start, 16), size)
+
+    def w_rows(index, start=0, size=FS):
+        return pl.ds(pl.multiple_of(index * FP + start, 16), size)
 
     f_devs = [{"fsdp": lax.rem(f + i, 2 * Y_RING)} for i in range(1, 2 * Y_RING)]
     z_devs = [z_dev[1], z_dev[-1], l_dev]
@@ -117,16 +124,18 @@
     def _():
         dy_all[t_rows(t), :] = dy_ref[...].T
 
-    mine_w = f_rows(f)
+    mine_w, left_w = w_rows(f), w_rows(f, FS, LEFT)
     w_all[mine_w, 0:MAIN] = gate_ref[:, 0:MAIN]
     w_all[mine_w, MAIN : 2 * MAIN] = up_ref[:, 0:MAIN]
     w_all[mine_w, 2 * MAIN : GU] = jnp.concatenate(
-        [gate_ref[:, MAIN:], up_ref[:, MAIN:], jnp.zeros((FS, 128 - 2 * TAIL), BF16)], axis=1
+        [gate_ref[:, MAIN:], up_ref[:, MAIN:], down_ref[:, MAIN : DH - LEFT]], axis=1
     )
-    w_all[mine_w, GU : GU + MAIN] = down_ref[:, 0:MAIN]
-    w_all[mine_w, GU + MAIN : PW] = jnp.concatenate(
-        [down_ref[:, MAIN:], jnp.zeros((FS, 128 - TAIL), BF16)], axis=1
+    w_all[mine_w, GU:PW] = down_ref[:, 0:MAIN]
+    turned = jnp.concatenate([down_ref[:, MAIN:], jnp.zeros((FS, 128 - TAIL), BF16)], axis=1).T
+    w_all[left_w, 0:MAIN] = jnp.concatenate(
+        [turned[TAIL - LEFT : TAIL, :], jnp.zeros((LEFT, MAIN - FS), BF16)], axis=1
     )
+    w_all[left_w, MAIN : 2 * MAIN] = jnp.zeros((LEFT, MAIN), BF16)
     pl.semaphore_wait(barrier, len(peers))
 
     def copy(src, dst, send, recv, i, device):
@@ -192,16 +201,17 @@
             self.first = 12 * p
             self.send = ws_sem.at[p]
             self.lanes = pl.ds(*LANES[p])
+            self.size = SHARD[p]
 
         def copy(self, block, rows, i, device):
-            at = w_all.at[f_rows(block, *rows), self.lanes]
+            at = w_all.at[w_rows(block, *rows), self.lanes]
             return copy(at, at, self.send, wr_sem, self.first + i, device)
 
         def full(self, way, back=0):
-            return self.copy(at_y(-back * way), (0, FS), 0 if way > 0 else 1, y_dev[way])
+            return self.copy(at_y(-back * way), (0, self.size), 0 if way > 0 else 1, y_dev[way])
 
         def half(self, way, back=1):
-            rows = (0, FS // 2) if way > 0 else (FS // 2, FS // 2)
+            rows = (0, FS // 2) if way > 0 else (FS // 2, self.size - FS // 2)
             return self.copy(at_y(-back * way), rows, 2 if way > 0 else 3, y_dev[way])
 
         def far(self, way, back=0):
@@ -212,10 +222,10 @@
             return self.copy(at_y(-back * way, True), rows, 6 if way > 0 else 7, y_dev[way])
 
         def over(self, incoming=False):
-            return self.copy(at_y(0, incoming), (0, FS), 8, x_dev)
+            return self.copy(at_y(0, incoming), (0, self.size), 8, x_dev)
 
         def late(self, i, incoming=False):
-            return self.copy(at_y((-1, 1, 2)[i], incoming), (PA, PB), 9 + i, x_dev)
+            return self.copy(at_y((-1, 1, 2)[i], incoming), (PA, self.size - PA), 9 + i, x_dev)
 
         def begin(self):
             self.over().start()
@@ -251,7 +261,7 @@
             self.late(2, True).wait_recv()
 
         def drain(self):
-            rows = 3 * FS + FS + 3 * PA + 3 * PB
+            rows = 7 * self.size
             block = w_all.at[pl.ds(0, rows), self.lanes]
             copy(block, block, self.send, wr_sem, 0, x_dev).wait_send()
 
@@ -291,9 +301,14 @@
 
     def turn(block):
         cols = block_cols(block)
+        one = lax.rem(block, Y_RING) * 2
         for i in range(PW // 128):
             lanes = slice(i * 128, (i + 1) * 128)
-            w_t[lanes, cols] = w_all[cols, lanes].T
+            both = jnp.concatenate([w_all[w_rows(one), lanes], w_all[w_rows(one + 1), lanes]], axis=0)
+            w_t[lanes, cols] = both.T
+        w_t[PW:, cols] = jnp.concatenate(
+            [w_all[w_rows(one, FS, LEFT), 0:FS], w_all[w_rows(one + 1, FS, LEFT), 0:FS]], axis=1
+        )
 
     def gate_up(block, first):
         cols = block_cols(block)
@@ -304,20 +319,21 @@
             value = dot(w_t[rows, cols], n_all[cols, :])
             gu[rows, :] = value if first else gu[rows, :] + value
 
-    spans = ((0, MAIN, MAIN, 0), (2 * MAIN, 2 * MAIN + TAIL, TAIL, MAIN))
-
-    def factors(gate_at, up_at, size, at):
-        gate, up = gu[gate_at : gate_at + size, :], gu[up_at : up_at + size, :]
-        sig = jax.nn.sigmoid(gate)
-        silu = gate * sig
-        hid[at : at + size, :] = (silu * up).astype(BF16)
-        fac[gate_at : gate_at + size, :] = up * sig * (1.0 + gate * (1.0 - sig))
-        fac[up_at : up_at + size, :] = silu
+    spans = (
+        (0, MAIN, MAIN, 128, TAIL - LEFT),
+        (2 * MAIN, 2 * MAIN + TAIL, TAIL - LEFT, 128 - TAIL + LEFT, 0),
+        (2 * MAIN + TAIL - LEFT, 2 * MAIN + 2 * TAIL - LEFT, LEFT, 128 + MAIN, DH - LEFT),
+    )
 
     def all_factors():
-        for span in spans:
-            factors(*span)
-        hid[MAIN + TAIL :, :] = jnp.zeros((DN - MAIN - TAIL, TOK), BF16)
+        for gate_at, up_at, size, at, _ in spans:
+            gate, up = gu[gate_at : gate_at + size, :], gu[up_at : up_at + size, :]
+            sig = jax.nn.sigmoid(gate)
+            silu = gate * sig
+            hid[at : at + size, :] = (silu * up).astype(BF16)
+            fac[gate_at : gate_at + size, :] = up * sig * (1.0 + gate * (1.0 - sig))
+            fac[up_at : up_at + size, :] = silu
+        hid[: 128 - TAIL + LEFT, :] = jnp.zeros((128 - TAIL + LEFT, TOK), BF16)
         act[GU - 32 :, :] = jnp.zeros((32, TOK), BF16)
 
     def handed(q):
@@ -334,7 +350,7 @@
 
     def hidden_back(block):
         cols = pl.ds(pl.multiple_of(lax.rem(block, Z_RING // 2) * 4 * LW, 128), 4 * LW)
-        return dot(w_t[GU:, cols], dy_all[cols, :])
+        return dot(w_t[GU - TAIL + LEFT :, cols], dy_all[cols, :])
 
     def back_first():
         d_hid[...] = hidden_back(lax.div(z, 2))
@@ -343,7 +359,7 @@
         def _(i):
             d_hid[...] += hidden_back(lax.div(z, 2) + 1 + 2 * i)
 
-    def back(gate_at, up_at, size, at):
+    def back(gate_at, up_at, size, _, at):
         grad = d_hid[at : at + size, :]
         d_gate = (grad * fac[gate_at : gate_at + size, :]).astype(BF16)
         d_up = (grad * fac[up_at : up_at + size, :]).astype(BF16)
@@ -357,10 +373,11 @@
 
     def back_last():
         d_hid[...] += hidden_back(lax.div(z, 2) + 2)
-        stat[...] = back(*spans[0]) + back(*spans[1])
+        stat[...] = back(*spans[0]) + back(*spans[1]) + back(*spans[2])
 
     def partial(off, j):
-        rows = t_rows(at_z(off, j == 1))
+        index = at_z(off, j == 1)
+        rows = w_rows(lax.div(index, 2), lax.rem(index, 2) * LW, LW)
         return dot(w_all[rows, :GU], act[...])
 
     row_id = lax.broadcasted_iota(jnp.int32, (STAT, TOK), 0)
@@ -463,8 +480,7 @@
         for one in gains:
             one.start()
 
-    A_ROWS, B_ROWS = (0, PA), (PA, PB)
-    AH, BH = PA // 2, PB // 2
+    AH, BH = PA // 2, (FS - PA) // 2
     h_rows = {1: lambda n: pl.ds(0, n), -1: lambda n: pl.ds(n, n)}
 
     class Grads:
@@ -472,14 +488,21 @@
             self.p, self.first, self.send = p, 15 * p, gs_sem.at[p]
             self.start, self.width = LANES[p]
             self.lanes = pl.ds(self.start, self.width)
-
-        def part(self, block, rows):
-            at = f_rows(block, *rows)
-            if self.p == 0:
-                return dot_t(n_all[at, :], act[: 2 * MAIN, :])
-            return jnp.concatenate(
-                [dot_t(n_all[at, :], act[2 * MAIN :, :]), dot_t(dy_all[at, :], hid[...])], axis=1
-            )
+            self.pb = SHARD[p] - PA
+            self.b_rows = {1: pl.ds(0, BH), -1: pl.ds(BH, self.pb - BH)}
+
+        def part(self, block, a):
+            at = f_rows(block, 0, PA) if a else f_rows(block, PA, FS - PA)
+            if self.p:
+                tails = dot_t(n_all[at, :], act[2 * MAIN :, :])
+                rest = dot_t(dy_all[at, :], hid[: 128 + MAIN, :])
+                return jnp.concatenate([tails + rest[:, :128], rest[:, 128:]], axis=1)
+            value = dot_t(n_all[at, :], act[: 2 * MAIN, :])
+            if a:
+                return value
+            left = dot_t(hid[128 + MAIN :, :], dy_all[f_rows(block), :])
+            left = jnp.concatenate([left, jnp.zeros((LEFT, 2 * MAIN - FS), F32)], axis=1)
+            return jnp.concatenate([value, left], axis=0)
 
         def copy(self, src, dst, index, i, device):
             index = (*index, self.lanes)
@@ -500,35 +523,35 @@
             return self.copy(afs, afr, (i, self.all(2), h_rows[way](AH)), 13 + i, y_dev[way])
 
         def b_over(self, o):
-            return self.copy(bxs, bxr, (o, self.all(PB)), 4 + o, x_dev)
+            return self.copy(bxs, bxr, (o, self.all(self.pb)), 4 + o, x_dev)
 
         def b_half(self, way):
-            return self.copy(bhs, bhr, (h_rows[way](BH),), 8 if way > 0 else 9, y_dev[way])
+            return self.copy(bhs, bhr, (self.b_rows[way],), 8 if way > 0 else 9, y_dev[way])
 
         def b_full(self, way):
             i = 0 if way > 0 else 1
-            return self.copy(bfs, bfr, (i, self.all(PB)), 10 + i, y_dev[way])
+            return self.copy(bfs, bfr, (i, self.all(self.pb)), 10 + i, y_dev[way])
 
         def a_over(self):
             return self.copy(axs, axr, (self.all(PA),), 12, x_dev)
 
         def begin(self):
             for n in (0, 1):
-                ahs[n, :, self.lanes] = self.part(at_y(2, n == 1), A_ROWS).astype(BF16)
+                ahs[n, :, self.lanes] = self.part(at_y(2, n == 1), True).astype(BF16)
             for way in WAYS:
                 self.a_half(way).start()
 
         def begin_rest(self, way):
             i = 0 if way > 0 else 1
             for n in (0, 1):
-                value = self.part(at_y(way, n == 1), A_ROWS)
+                value = self.part(at_y(way, n == 1), True)
                 own[i, n, :, self.lanes] = value[:AH] if way > 0 else value[AH:]
                 rest = value[AH:] if way > 0 else value[:AH]
                 afs[i, n, h_rows[-way](AH), self.lanes] = rest.astype(BF16)
             self.a_rest(way).start()
 
         def send_over(self, o):
-            bxs[o, :, self.lanes] = self.part(at_y(o, True), B_ROWS).astype(BF16)
+            bxs[o, : self.pb, self.lanes] = self.part(at_y(o, True), False).astype(BF16)
             self.b_over(o).start()
 
         def a_next(self, way):
@@ -542,10 +565,10 @@
 
         def crossed(self, o):
             self.b_over(o).wait_recv()
-            return self.part(at_y(o), B_ROWS) + bxr[o, :, self.lanes].astype(F32)
+            return self.part(at_y(o), False) + bxr[o, : self.pb, self.lanes].astype(F32)
 
         def b_next(self):
-            bhs[:, self.lanes] = self.crossed(2).astype(BF16)
+            bhs[: self.pb, self.lanes] = self.crossed(2).astype(BF16)
             for way in WAYS:
                 self.b_half(way).start()
 
@@ -553,8 +576,7 @@
             i = 0 if way > 0 else 1
             value = self.crossed(1 if way > 0 else 3)
             self.b_half(way).wait_recv()
-            rows = h_rows[way](BH)
-            other = h_rows[-way](BH)
+            rows, other = self.b_rows[way], self.b_rows[-way]
             mine = value[:BH] if way > 0 else value[BH:]
             rest = value[BH:] if way > 0 else value[:BH]
             bfs[i, rows, self.lanes] = (mine + bhr[rows, self.lanes].astype(F32)).astype(BF16)
@@ -563,7 +585,7 @@
 
         def a_sum(self, n):
             return (
-                self.part(at_y(0, n == 1), A_ROWS)
+                self.part(at_y(0, n == 1), True)
                 + afr[0, n, :, self.lanes].astype(F32) + afr[1, n, :, self.lanes].astype(F32)
             )
 
@@ -581,10 +603,10 @@
         def arrived_b(self):
             for way in WAYS:
                 self.b_full(way).wait_recv()
-            return bfr[0, :, self.lanes].astype(F32) + bfr[1, :, self.lanes].astype(F32)
+            return bfr[0, : self.pb, self.lanes].astype(F32) + bfr[1, : self.pb, self.lanes].astype(F32)
 
         def drain(self):
-            rows = 2 * PA + 4 * PA + 4 * PB + PB + 2 * PB + PA
+            rows = 7 * PA + 7 * self.pb
             block = w_all.at[pl.ds(0, rows), self.lanes]
             copy(block, block, self.send, gr_sem, 0, x_dev).wait_send()
 
@@ -595,12 +617,21 @@
             ref[rows, lanes] = ref[rows, lanes] + part if add else part
 
         if p == 0:
-            put(gate_grad, slice(0, MAIN), value[:, :MAIN])
-            put(up_grad, slice(0, MAIN), value[:, MAIN:])
+            size = rows.stop - rows.start
+            put(gate_grad, slice(0, MAIN), value[:size, :MAIN])
+            put(up_grad, slice(0, MAIN), value[:size, MAIN:])
+            if value.shape[0] > size:
+                more = value[size:, :MAIN]
+                more = left_sum[...] + more if add else more
+                left_sum[...] = more
+                if add:
+                    wide_left = jnp.concatenate([more, jnp.zeros((128 - LEFT, MAIN), F32)], axis=0).T
+                    down_grad[:, DH - LEFT :] = wide_left[:FS, :LEFT]
         else:
             put(gate_grad, slice(MAIN, MAIN + TAIL), value[:, :TAIL])
             put(up_grad, slice(MAIN, MAIN + TAIL), value[:, TAIL : 2 * TAIL])
-            put(down_grad, slice(0, MAIN + TAIL), value[:, 128 : 128 + MAIN + TAIL])
+            put(down_grad, slice(MAIN, DH - LEFT), value[:, 2 * TAIL : 128])
+            put(down_grad, slice(0, MAIN), value[:, 128:])
 
     top, rest = slice(0, PA), slice(PA, FS)
     writes = [
@@ -758,28 +789,29 @@
             pltpu.VMEM((DM, TOK), BF16),
             pltpu.VMEM((DM, TOK), BF16),
             pltpu.VMEM((DM, TOK), BF16),
-            pltpu.VMEM((DM, PW), BF16),
-            pltpu.VMEM((PW, DM), BF16),
+            pltpu.VMEM((2 * Y_RING * FP, PW), BF16),
+            pltpu.VMEM((WT, DM), BF16),
             pltpu.VMEM((LW, TOK), BF16),
             pltpu.VMEM((DM, 128), F32),
             pltpu.VMEM((GU, TOK), F32),
             pltpu.VMEM((GU, TOK), F32),
-            pltpu.VMEM((DN, TOK), BF16),
+            pltpu.VMEM((HID, TOK), BF16),
             pltpu.VMEM((GU, TOK), BF16),
-            pltpu.VMEM((DN, TOK), F32),
+            pltpu.VMEM((DH, TOK), F32),
             pltpu.VMEM((1, TOK), F32),
             pltpu.VMEM((1, TOK), F32),
             pltpu.VMEM((LW, TOK), F32),
             pltpu.VMEM((1, TOK), F32),
+            pltpu.VMEM((LEFT, MAIN), F32),
             pltpu.VMEM((16, LW + STAT, TOK), BF16),
             pltpu.VMEM((16, LW + STAT, TOK), BF16),
             pltpu.VMEM((LW + STAT, TOK), BF16),
             pltpu.VMEM((LW + STAT, TOK), BF16),
             *(pltpu.VMEM((2, PA, PW), BF16),) * 2,
             *(pltpu.VMEM((2, 2, PA, PW), BF16),) * 2,
-            *(pltpu.VMEM((4, PB, PW), BF16),) * 2,
-            *(pltpu.VMEM((PB, PW), BF16),) * 2,
-            *(pltpu.VMEM((2, PB, PW), BF16),) * 2,
+            *(pltpu.VMEM((4, FP - PA, PW), BF16),) * 2,
+            *(pltpu.VMEM((FP - PA, PW), BF16),) * 2,
+            *(pltpu.VMEM((2, FP - PA, PW), BF16),) * 2,
             *(pltpu.VMEM((PA, PW), BF16),) * 2,
             pltpu.VMEM((2, 2, PA // 2, PW), F32),
             pltpu.VMEM((8, LW), F32),

time: 124 us -> 122 us (0.984)
  Pallas kernels: 123 us -> 121 us
    pallas_call x1, Pallas kernels: 120 us -> 118 us  [window(): pl.pallas_call(kernel, name='window', out_shape=shapes, in_specs=[hbm] *...]
where the time goes in v7:
time: 122 us
  Pallas kernels  121 us (99%)
    pallas_call x1, Pallas kernels, window(): pl.pallas_call(kernel, name='window', out_shape=shapes, in_specs=[hbm] *...  118 us
    pallas_call x1, Pallas kernels, window(): pl.pallas_call(write, name='write', out_shape=shapes, in_specs=[hbm] * 5,...  2.53 us

profile of v7, /device:TPU:8, one launch (start us, length us, event | category | flops | bytes accessed | tf_op | source)
XLA Modules:
  0.0 121.6 jit_solution(16545331354538204273)
XLA Ops:
  0.6 118.2 %window.1 = (bf16[512,160]{1,0:T(8,128)(2,1)}, f32[320,432]{1,0:T(8,128)}, f32[320,432]{1,0:T(8,128)}, f32[320,432]{1,0:T(8,128)}, f32[1,160]{1,0:T(1,128)}) custom-call(bf16[512,160]{1,0:T(8,128)(2,1)} %bitcast.16, bf16[512,160]{1,0:T(8,128)(2,1)} %bitcast.17, f32[1,2560]{1,0:T(1,128)} %gain_in.1, bf16[320,432]{1,0:T(8,128)(2,1)} %bitcast.13, ...), custom_call_target="tpu_custom_call" | custom-call | tf_op jit(solution)/shard_map/window/pallas_call | solution.py:778
  118.8 2.5 %write.1 = (bf16[512,160]{1,0:T(8,128)(2,1)}, f32[320,432]{1,0:T(8,128)}, f32[320,432]{1,0:T(8,128)}, f32[320,432]{1,0:T(8,128)}, f32[1,160]{1,0:T(1,128)}) custom-call(bf16[512,160]{1,0:T(8,128)(2,1)} %get-tuple-element.15.refs_0_, f32[320,432]{1,0:T(8,128)} %get-tuple-element.16.refs_1_, f32[320,432]{1,0:T(8,128)} %get-tuple-element.17.refs_2_, ...), custom_call_target="tpu_custom_call" | custom-call | tf_op jit(solution)/shard_map/write/pallas_call | solution.py:827

commit v8 on v7

--- a/solution.py
+++ b/solution.py
@@ -34,7 +34,7 @@
 
 ORDER = (
     (
-        "w0", "w1", "Xb", "cols", "Xz", "Wb0", "Xp", "X0.0", "X0.1", "Wb1", "Wo0", "Wn-0", "Wo1", "Wn+1",
+        "w0", "w1", "Xb", "Wb0", "cols", "Xz", "Xp", "X0.0", "X0.1", "Wb1", "Wo0", "Wn-0", "Wo1", "Wn+1",
         "Wn+0", "Wn-1", "Wm0", "X1.0", "X1.1", "X2.0", "WT0", "Wf-1", "Wf+0", "X2.1", "Wf-0", "WT-", "Wm1",
         "Tp", "Wf+1", "WT+", "T0.0", "X3.0", "X3.1", "N", "T0.1", "T1.0", "GU0", "T1.1", "WT2", "GU-", "GU2",
         "T2.0", "T2.1", "dH0", "GU+", "fac", "T3.0", "T3.1", "dH1", "z0", "ah0", "bx21", "z1a", "bx11",

time: 122 us -> 122 us (level)
  no operation moved by 1% of the time
where the time goes in v8:
time: 122 us; the launch traced here: 121 us
  Pallas kernels  120 us (98%)
    pallas_call x1, Pallas kernels, window(): pl.pallas_call(kernel, name='window', out_shape=shapes, in_specs=[hbm] *...  118 us
    pallas_call x1, Pallas kernels, window(): pl.pallas_call(write, name='write', out_shape=shapes, in_specs=[hbm] * 5,...  2.53 us

profile of v8, /device:TPU:8, one launch (start us, length us, event | category | flops | bytes accessed | tf_op | source)
XLA Modules:
  0.0 121.3 jit_solution(15751718598940340444)
XLA Ops:
  0.6 117.9 %window.1 = (bf16[512,160]{1,0:T(8,128)(2,1)}, f32[320,432]{1,0:T(8,128)}, f32[320,432]{1,0:T(8,128)}, f32[320,432]{1,0:T(8,128)}, f32[1,160]{1,0:T(1,128)}) custom-call(bf16[512,160]{1,0:T(8,128)(2,1)} %bitcast.16, bf16[512,160]{1,0:T(8,128)(2,1)} %bitcast.17, f32[1,2560]{1,0:T(1,128)} %gain_in.1, bf16[320,432]{1,0:T(8,128)(2,1)} %bitcast.13, ...), custom_call_target="tpu_custom_call" | custom-call | tf_op jit(solution)/shard_map/window/pallas_call | solution.py:778
  118.5 2.5 %write.1 = (bf16[512,160]{1,0:T(8,128)(2,1)}, f32[320,432]{1,0:T(8,128)}, f32[320,432]{1,0:T(8,128)}, f32[320,432]{1,0:T(8,128)}, f32[1,160]{1,0:T(1,128)}) custom-call(bf16[512,160]{1,0:T(8,128)(2,1)} %get-tuple-element.15.refs_0_, f32[320,432]{1,0:T(8,128)} %get-tuple-element.16.refs_1_, f32[320,432]{1,0:T(8,128)} %get-tuple-element.17.refs_2_, ...), custom_call_target="tpu_custom_call" | custom-call | tf_op jit(solution)/shard_map/write/pallas_call | solution.py:827
